TPU v7x, 256 devices: a whole 4x4x8 slice. The times are simulated.
256 devices in a mesh: member: 16 (over y_lo, x, core), dp: 16 (over z, y_hi).
Axes of the slice: x: 4, y: 4 (y_hi: 2, y_lo: 2; y = y_hi * 2 + y_lo), z: 8, core: 2. Of those that a mesh axis runs over, the one named last changes fastest.
Arguments:
- trunk: bfloat16 [6304, 1024], P('dp'), may hold values from -6 to 6
- normgain: float32 [1024], replicated, may hold values from 0.25 to 1.75
- expand: bfloat16 [1024, 2048], P('member'), may hold values from -0.1875 to 0.1875
- shrink: bfloat16 [2048, 1024], P('member'), may hold values from -0.125 to 0.125
- inscale: float32 [16, 1024], P('member'), may hold values from 0.25 to 1.75
- hidscale: float32 [16, 2048], P('member'), may hold values from 0.25 to 1.75
- actscale: float32 [16, 2048], P('member'), may hold values from 0.25 to 1.75
- outscale: float32 [16, 1024], P('member'), may hold values from 0.25 to 1.75
- cotangent: bfloat16 [16, 6304, 1024], P('member', 'dp'), may hold values from -6 to 6
Outputs:
- trunk_grad: bfloat16 [6304, 1024], P('dp', 'member')
- expand_grad: float32 [1024, 2048], P('member')
- shrink_grad: float32 [2048, 1024], P('member')
- inscale_grad: float32 [16, 1024], P('member')
- hidscale_grad: float32 [16, 2048], P('member')
- actscale_grad: float32 [16, 2048], P('member')
- outscale_grad: float32 [16, 1024], P('member')
- normgain_grad: float32 [1024], replicated
All inputs are finite; a program needn't handle non-finite values.
Results may differ from a plain program's by a relative error of at most 0.024.
Values may be sent and summed in bfloat16 or wider, within the bound.
A program may use at most 64 MiB of HBM per device.

v0:
```python
import jax
import jax.numpy as jnp
from jax import lax
from jax.sharding import Mesh
from jax.sharding import PartitionSpec as P

MEMBER = ("member_0", "member_1", "member_2")


eps = 1e-06
coeff = 0.7978845608028654


def sent_to_all(x, axis):
    copies = jnp.broadcast_to(x, (lax.axis_size(axis), *x.shape))
    return lax.all_to_all(copies, axis, split_axis=0, concat_axis=0, tiled=True)


def joined_along(tiles, dim):
    tiles = jnp.moveaxis(tiles, 0, dim)
    dims = tiles.shape
    return tiles.reshape(*dims[:dim], dims[dim] * dims[dim + 1], *dims[dim + 2 :])


def gathered_by_axis(x, axes, dim):
    far, near = axes
    tiles = sent_to_all(sent_to_all(x, far), near)
    return joined_along(tiles.swapaxes(0, 1).reshape(-1, *x.shape), dim)


def split_up(x, dim, peers):
    before, after = (x.shape[:dim], x.shape[dim + 1 :])
    return jnp.moveaxis(x.reshape(*before, peers, -1, *after), dim, 0)


def sent_and_summed(x, axis, dim):
    tiles = split_up(x, dim, lax.axis_size(axis))
    arrived = lax.all_to_all(tiles, axis, split_axis=0, concat_axis=0, tiled=True)
    return arrived.astype(jnp.float32).sum(axis=0)


def summed_rows(x, axes, dim):
    far, near = axes
    tiles = split_up(x, dim, lax.axis_size(far))
    nearer = sent_and_summed(tiles, near, dim + 1)
    arrived = lax.all_to_all(
        nearer.astype(jnp.bfloat16), far, split_axis=0, concat_axis=0, tiled=True
    )
    return arrived.astype(jnp.float32).sum(axis=0)


def filled_up(lines, peers):
    spare = -len(lines) % peers
    return jnp.pad(lines, [(0, spare)] + [(0, 0)] * (lines.ndim - 1))


def collect(x, axis, dim):
    return joined_along(sent_to_all(x, axis), dim)


def sum_by_parts(x, axes):
    lines = x.reshape(-1, x.shape[-1])
    own = sent_and_summed(filled_up(lines, lax.axis_size(axes)), axes, 0)
    whole = collect(own.astype(jnp.bfloat16), axes, 0)
    return whole[: len(lines)].reshape(x.shape).astype(jnp.float32)


def over_copies(x, axis):
    return sent_to_all(x, axis).sum(axis=0)


def in_one(arrays, axis):
    ends = [0]
    for a in arrays:
        ends.append(ends[-1] + a.size)
    total = over_copies(jnp.concatenate([a.ravel() for a in arrays]), axis)
    return tuple((total[b:e].reshape(a.shape) for a, b, e in zip(arrays, ends, ends[1:])))


def gelu_pair(hidden):
    inner = coeff * (hidden + 0.044715 * hidden * hidden * hidden)
    tangent = jnp.tanh(inner)
    active = 0.5 * hidden * (1.0 + tangent)
    slope = 0.5 * (1.0 + tangent) + 0.5 * hidden * (1.0 - tangent * tangent) * coeff * (
        1.0 + 3.0 * 0.044715 * hidden * hidden
    )
    return (active, slope)


def rounded_term(left, right):
    term = lax.dot_general(
        left, right, (((0,), (0,)), ((), ())), preferred_element_type=jnp.float32
    )
    return lax.optimization_barrier(term.astype(jnp.bfloat16)).astype(jnp.float32)


def body(trunk, normgain, expand, shrink, inscale, hidscale, actscale, outscale, cotangent):
    scale_in = inscale[0]
    scale_hid = hidscale[0]
    scale_act = actscale[0]
    scale_out = outscale[0]
    tokens = trunk.astype(jnp.float32)
    centered = tokens - jnp.mean(tokens, axis=1, keepdims=True)
    variance = jnp.mean(centered * centered, axis=1, keepdims=True)
    inv_std = lax.rsqrt(variance + eps)
    normed = centered * inv_std
    gained = normed * normgain
    scaled_in = (gained * scale_in).astype(jnp.bfloat16)
    expand_full = lax.all_gather(expand, MEMBER, axis=0, tiled=True)
    project = jnp.dot(scaled_in, expand_full, preferred_element_type=jnp.float32)
    hidden = project * scale_hid
    active, slope = gelu_pair(hidden)
    scaled_act = (active * scale_act).astype(jnp.bfloat16)
    upstream = cotangent[0].astype(jnp.float32)
    scaled_cot = (upstream * scale_out).astype(jnp.bfloat16)
    piece = gathered_by_axis(shrink, (("member_0", "member_1"), "member_2"), 0)
    second = jnp.dot(scaled_act, piece, preferred_element_type=jnp.float32)
    back = lax.dot_general(
        scaled_cot, piece, (((1,), (1,)), ((), ())), preferred_element_type=jnp.float32
    )
    back_act = back
    second, back_act = (second, back_act)
    grad_out = jnp.sum(upstream * second, axis=0)
    grad_act = jnp.sum(back_act * active, axis=0)
    back_hidden = back_act * scale_act * slope
    grad_hid = jnp.sum(back_hidden * project, axis=0)
    back_proj = (back_hidden * scale_hid).astype(jnp.bfloat16)
    expand_part = summed_rows(
        rounded_term(scaled_in, back_proj).astype(jnp.bfloat16),
        (("member_0", "member_1"), "member_2"),
        0,
    )
    shrink_part = summed_rows(
        rounded_term(scaled_act, scaled_cot).astype(jnp.bfloat16),
        (("member_0", "member_1"), "member_2"),
        0,
    )
    expand_grad, shrink_grad = (
        sum_by_parts(expand_part.astype(jnp.bfloat16), "dp"),
        sum_by_parts(shrink_part.astype(jnp.bfloat16), "dp"),
    )
    back_norm = lax.dot_general(
        back_proj, expand_full, (((1,), (1,)), ((), ())), preferred_element_type=jnp.float32
    )
    grad_in = jnp.sum(back_norm * gained, axis=0)
    back_scaled = back_norm * scale_in
    gain_term = jnp.sum(back_scaled * normed, axis=0)
    back_unit = back_scaled * normgain
    back_trunk = inv_std * (
        back_unit
        - jnp.mean(back_unit, axis=1, keepdims=True)
        - normed * jnp.mean(back_unit * normed, axis=1, keepdims=True)
    )
    member_term = upstream + back_trunk
    trunk_grad = sent_and_summed(member_term.astype(jnp.bfloat16), MEMBER, 1).astype(jnp.bfloat16)
    grad_in, grad_hid, grad_act, grad_out, gain_shard = in_one(
        (grad_in, grad_hid, grad_act, grad_out, gain_term), "dp"
    )
    gain_grad = over_copies(gain_shard, MEMBER)
    return (
        trunk_grad,
        expand_grad,
        shrink_grad,
        grad_in[None],
        grad_hid[None],
        grad_act[None],
        grad_out[None],
        gain_grad,
    )


def solution(mesh):
    finer = Mesh(
        mesh.devices.reshape(2, 4, 2, mesh.shape["dp"]), ("member_0", "member_1", "member_2", "dp")
    )
    in_specs = (
        P("dp", None),
        P(),
        P(MEMBER, None),
        P(MEMBER, None),
        P(MEMBER, None),
        P(MEMBER, None),
        P(MEMBER, None),
        P(MEMBER, None),
        P(MEMBER, "dp", None),
    )
    out_specs = (
        P("dp", MEMBER),
        P(MEMBER, None),
        P(MEMBER, None),
        P(MEMBER, None),
        P(MEMBER, None),
        P(MEMBER, None),
        P(MEMBER, None),
        P(),
    )
    return jax.shard_map(body, mesh=finer, in_specs=in_specs, out_specs=out_specs, check_vma=False)
```

profile of v0, /device:TPU:1, one launch (start us, length us, event | category | flops | bytes accessed | tf_op | source)
XLA Modules:
  0.0 313.7 jit_solution(12734090389983294515)
XLA Ops:
  7.2 0.0 all-gather.2.cloned.1.call-start
  7.2 0.7 all-gather.2.cloned.1.call-update
  7.9 2.6 broadcast_in_dim.36
  10.5 5.9 %all-to-all-start = ((bf16[8,128,1024]{2,1,0:T(8,128)(2,1)}), bf16[8,128,1024]{2,1,0:T(8,128)(2,1)S(1)}, u32[]{:S(2)}, u32[]{:S(2)}) async-start(bf16[8,128,1024]{2,1,0:T(8,128)(2,1)} %broadcast_in_dim.36), calls=%async_computation | async-start | bytes 4194304 | tf_op jit(solution)/shard_map/all_to_all | solution.py:16
  16.4 0.0 copy-done.1
  16.4 0.2 convert_reduce_fusion
  16.6 0.4 fusion.23
  17.0 26.6 %all-to-all-done = bf16[8,128,1024]{2,1,0:T(8,128)(2,1)S(1)} async-done(((bf16[8,128,1024]{2,1,0:T(8,128)(2,1)}), bf16[8,128,1024]{2,1,0:T(8,128)(2,1)S(1)}, u32[]{:S(2)}, u32[]{:S(2)}) %all-to-all-start) | async-done | bytes 2097184 | tf_op jit(solution)/shard_map/all_to_all | solution.py:16
  43.5 0.5 broadcast_in_dim.37
  44.1 8.8 %all_to_all.67 = bf16[2,8,128,1024]{3,2,1,0:T(8,128)(2,1)S(1)} all-to-all(bf16[2,8,128,1024]{3,2,1,0:T(8,128)(2,1)S(1)} %broadcast_in_dim.37), channel_id=1, replica_groups=mesh['member_0'=2,'member_1'=4,'member_2'=2,'dp'=16] {'member_2'}, dimensions={0} | all-to-all | bytes 8388608 | tf_op jit(solution)/shard_map/all_to_all | solution.py:16
  52.8 2.4 copy.27
  55.2 11.8 %all-gather.2.cloned.1.call-done = bf16[1024,2048]{1,0:T(8,128)(2,1)} async-done(((bf16[64,2048]{1,0:T(8,128)(2,1)}), bf16[1024,2048]{1,0:T(8,128)(2,1)}) %all-gather.2.cloned.1.call-update) | async-done | bytes 4194320 | tf_op jit(solution)/shard_map/all_gather | solution.py:109
  67.1 0.0 copy-start.7
  67.1 0.0 copy-start.8
  67.1 4.3 %fusion.37 = f32[394,2048]{1,0:T(8,128)S(1)} fusion(bf16[1024,2048]{1,0:T(8,128)(2,1)} %all-gather.2.cloned.1.call-done, bf16[394,1024]{1,0:T(8,128)(2,1)S(1)} %copy-done.1, f32[1024]{0:T(1024)S(1)} %bitcast.60, f32[1024]{0:T(1024)S(1)} %copy-done.5, f32[394]{0:T(512)S(1)} %add_rsqrt_fusion, f32[394]{0:T(512)S(1)} %broadcast_multiply_fusion.2), kind=kOutput, calls=%fused_computation.60 | convolution fusion | flops 1654976512 | bytes 8240208 | tf_op jit(solution)/shard_map/dot_general | solution.py:110
  71.5 0.0 copy-start.9
  71.5 2.4 fusion.26
  73.9 4.2 %multiply_reduce_fusion = (f32[2048]{0:T(1024)S(1)}, f32[2048]{0:T(1024)S(1)}, f32[394,2048]{1,0:T(8,128)S(1)}) fusion(f32[394,2048]{1,0:T(8,128)S(1)} %fusion.37, f32[2048]{0:T(1024)S(1)} %bitcast.65, f32[2048]{0:T(1024)S(1)} %bitcast.70, bf16[2048,1024]{1,0:T(8,128)(2,1)S(1)} %bitcast.55, bf16[1,394,1024]{2,1,0:T(8,128)(2,1)S(1)} %copy-done.3, ...), kind=kOutput, calls=%fused_computation.12 | convolution fusion | flops 1673934848 | bytes 11493376 | tf_op jit(solution)/shard_map/dot_general | solution.py:118
  78.1 5.0 %convolution_convert_fusion = bf16[2048,1024]{1,0:T(8,128)(2,1)} fusion(bf16[1,394,1024]{2,1,0:T(8,128)(2,1)S(1)} %copy-done.3, f32[1024]{0:T(1024)S(1)} %bitcast.75, f32[2048]{0:T(1024)S(1)} %bitcast.71, f32[394,2048]{1,0:T(8,128)S(1)} %fusion.37, f32[2048]{0:T(1024)S(1)} %bitcast.66), kind=kOutput, calls=%fused_computation.4 | convolution fusion | flops 1664739328 | bytes 8249344 | tf_op jit(solution)/shard_map/dot_general | solution.py:91
  83.1 4.5 %convolution_convert_fusion.1 = bf16[1024,2048]{1,0:T(8,128)(2,1)S(1)} fusion(f32[2048]{0:T(1024)S(1)} %bitcast.67, bf16[394,1024]{1,0:T(8,128)(2,1)S(1)} %copy-done.1, f32[1024]{0:T(1024)S(1)} %bitcast.61, f32[1024]{0:T(1024)S(1)} %copy-done.5, f32[394]{0:T(512)S(1)} %add_rsqrt_fusion, f32[394]{0:T(512)S(1)} %broadcast_multiply_fusion.2, ...), kind=kOutput, calls=%fused_computation.5 | convolution fusion | flops 1674825728 | bytes 11484240 | tf_op jit(solution)/shard_map/dot_general | solution.py:91
  87.6 5.2 %fusion.22 = (f32[1024]{0:T(1024)S(1)}, f32[394]{0:T(512)S(1)}, f32[1024]{0:T(1024)S(1)}, f32[394]{0:T(512)S(1)}, f32[394,1024]{1,0:T(8,128)}) fusion(bf16[394,1024]{1,0:T(8,128)(2,1)S(1)} %copy-done.1, f32[1024]{0:T(1024)S(1)} %bitcast.62, f32[394]{0:T(512)S(1)} %add_rsqrt_fusion, f32[394]{0:T(512)S(1)} %broadcast_multiply_fusion.2, ...), kind=kOutput, calls=%fused_computation.37 | convolution fusion | flops 1675549952 | bytes 13109408 | tf_op jit(solution)/shard_map/dot_general | solution.py:142
  92.8 2.3 copy.45
  95.1 5.9 %all-to-all-start.3 = ((bf16[2,8,64,2048]{3,2,1,0:T(8,128)(2,1)}), bf16[2,8,64,2048]{3,2,1,0:T(8,128)(2,1)}, u32[]{:S(2)}, u32[]{:S(2)}) async-start(bf16[2,8,64,2048]{3,2,1,0:T(8,128)(2,1)} %bitcast.50), calls=%async_computation.3 | async-start | bytes 8388608 | tf_op jit(solution)/shard_map/all_to_all | solution.py:38
  101.0 4.7 %copy.44 = bf16[8,2,128,1024]{3,2,0,1:T(8,128)(2,1)} copy(bf16[8,2,128,1024]{3,2,1,0:T(8,128)(2,1)} %bitcast.52) | data formatting | bytes 8388608 | tf_op jit(solution)/shard_map/reshape;reshape | solution.py:33
  105.7 0.0 all-to-all-done.3
  105.7 11.5 %all_to_all.68 = bf16[2,8,128,1024]{3,2,1,0:T(8,128)(2,1)} all-to-all(bf16[2,8,128,1024]{3,2,1,0:T(8,128)(2,1)} %bitcast.51), channel_id=1, replica_groups=mesh['member_0'=2,'member_1'=4,'member_2'=2,'dp'=16] {'member_2'}, dimensions={0} | all-to-all | bytes 8388608 | tf_op jit(solution)/shard_map/all_to_all | solution.py:38
  117.3 1.0 broadcast_in_dim.40
  118.3 11.0 %all-to-all-start.11 = ((f32[16,1,7168]{2,1,0:T(1,128)}), f32[16,1,7168]{2,1,0:T(1,128)S(1)}, u32[]{:S(2)}, u32[]{:S(2)}) async-start(f32[16,1,7168]{2,1,0:T(1,128)} %broadcast_in_dim.40), calls=%async_computation.11 | async-start | bytes 917504 | tf_op jit(solution)/shard_map/all_to_all | solution.py:16
  129.2 2.2 fusion.24
  131.4 1.4 copy.28
  132.8 12.6 %all-to-all-done.11 = f32[16,1,7168]{2,1,0:T(1,128)S(1)} async-done(((f32[16,1,7168]{2,1,0:T(1,128)}), f32[16,1,7168]{2,1,0:T(1,128)S(1)}, u32[]{:S(2)}, u32[]{:S(2)}) %all-to-all-start.11) | async-done | bytes 458784 | tf_op jit(solution)/shard_map/all_to_all | solution.py:16
  145.4 6.0 %all-to-all-start.2 = ((bf16[16,394,64]{1,2,0:T(8,128)(2,1)}), bf16[16,394,64]{1,2,0:T(8,128)(2,1)S(1)}, u32[]{:S(2)}, u32[]{:S(2)}) async-start(bf16[16,394,64]{1,2,0:T(8,128)(2,1)} %bitcast.9), calls=%async_computation.2 | async-start | bytes 2097152 | tf_op jit(solution)/shard_map/all_to_all | solution.py:38
  151.4 0.3 reduce_sum.199
  151.7 0.6 fusion.41
  152.3 15.0 %all-to-all-done.2 = bf16[16,394,64]{1,2,0:T(8,128)(2,1)S(1)} async-done(((bf16[16,394,64]{1,2,0:T(8,128)(2,1)}), bf16[16,394,64]{1,2,0:T(8,128)(2,1)S(1)}, u32[]{:S(2)}, u32[]{:S(2)}) %all-to-all-start.2) | async-done | bytes 806944 | tf_op jit(solution)/shard_map/all_to_all | solution.py:38
  167.3 0.7 broadcast_in_dim.45
  168.0 4.1 %all-to-all-start.12 = ((f32[16,1,1024]{2,1,0:T(1,128)}), f32[16,1,1024]{2,1,0:T(1,128)S(1)}, u32[]{:S(2)}, u32[]{:S(2)}) async-start(f32[16,1,1024]{2,1,0:T(1,128)} %broadcast_in_dim.45), calls=%async_computation.12 | async-start | bytes 131072 | tf_op jit(solution)/shard_map/all_to_all | solution.py:16
  172.0 5.2 %reduce_sum.188 = bf16[8,64,2048]{2,1,0:T(8,128)(2,1)} reduce(bf16[2,8,64,2048]{3,2,1,0:T(8,128)(2,1)} %all-to-all-done.3, bf16[]{:T(256)} %constant.28.clone.1), dimensions={0}, to_apply=%region_5.0 | reduce | flops 1048576 | bytes 6291458 | tf_op jit(solution)/shard_map/reduce_sum | solution.py:39
  177.2 0.7 all-to-all-done.12
  177.9 4.4 %all-to-all-start.4 = ((bf16[8,64,2048]{2,1,0:T(8,128)(2,1)}), bf16[8,64,2048]{2,1,0:T(8,128)(2,1)S(1)}, u32[]{:S(2)}, u32[]{:S(2)}) async-start(bf16[8,64,2048]{2,1,0:T(8,128)(2,1)} %reduce_sum.188), calls=%async_computation.4 | async-start | bytes 4194304 | tf_op jit(solution)/shard_map/all_to_all | solution.py:46
  182.3 5.2 %reduce_sum.191 = bf16[8,128,1024]{2,1,0:T(8,128)(2,1)} reduce(bf16[2,8,128,1024]{3,2,1,0:T(8,128)(2,1)} %all_to_all.68, bf16[]{:T(256)} %constant.28.clone.1), dimensions={0}, to_apply=%region_8.0 | reduce | flops 1048576 | bytes 6291458 | tf_op jit(solution)/shard_map/reduce_sum | solution.py:39
  187.5 21.9 %all-to-all-done.4 = bf16[8,64,2048]{2,1,0:T(8,128)(2,1)S(1)} async-done(((bf16[8,64,2048]{2,1,0:T(8,128)(2,1)}), bf16[8,64,2048]{2,1,0:T(8,128)(2,1)S(1)}, u32[]{:S(2)}, u32[]{:S(2)}) %all-to-all-start.4) | async-done | bytes 2097184 | tf_op jit(solution)/shard_map/all_to_all | solution.py:46
  209.4 1.3 copy-done
  210.7 6.1 %all-to-all-start.8 = ((bf16[8,128,1024]{2,1,0:T(8,128)(2,1)}), bf16[8,128,1024]{2,1,0:T(8,128)(2,1)S(1)}, u32[]{:S(2)}, u32[]{:S(2)}) async-start(bf16[8,128,1024]{2,1,0:T(8,128)(2,1)} %reduce_sum.191), calls=%async_computation.8 | async-start | bytes 4194304 | tf_op jit(solution)/shard_map/all_to_all | solution.py:46
  216.8 2.0 reduce_sum.189
  218.8 0.8 reshape.70
  219.6 24.3 %all-to-all-done.8 = bf16[8,128,1024]{2,1,0:T(8,128)(2,1)S(1)} async-done(((bf16[8,128,1024]{2,1,0:T(8,128)(2,1)}), bf16[8,128,1024]{2,1,0:T(8,128)(2,1)S(1)}, u32[]{:S(2)}, u32[]{:S(2)}) %all-to-all-start.8) | async-done | bytes 2097184 | tf_op jit(solution)/shard_map/all_to_all | solution.py:46
  243.9 3.5 %all-to-all-start.5 = ((bf16[16,4,2048]{2,1,0:T(4,128)(2,1)}), bf16[16,4,2048]{2,1,0:T(4,128)(2,1)S(1)}, u32[]{:S(2)}, u32[]{:S(2)}) async-start(bf16[16,4,2048]{2,1,0:T(4,128)(2,1)} %reshape.70), calls=%async_computation.5 | async-start | bytes 524288 | tf_op jit(solution)/shard_map/all_to_all | solution.py:38
  247.5 1.1 reduce_sum.192
  248.6 11.1 %all-to-all-done.5 = bf16[16,4,2048]{2,1,0:T(4,128)(2,1)S(1)} async-done(((bf16[16,4,2048]{2,1,0:T(4,128)(2,1)}), bf16[16,4,2048]{2,1,0:T(4,128)(2,1)S(1)}, u32[]{:S(2)}, u32[]{:S(2)}) %all-to-all-start.5) | async-done | bytes 262176 | tf_op jit(solution)/shard_map/all_to_all | solution.py:38
  259.7 3.5 %all-to-all-start.9 = ((bf16[16,8,1024]{2,1,0:T(8,128)(2,1)}), bf16[16,8,1024]{2,1,0:T(8,128)(2,1)S(1)}, u32[]{:S(2)}, u32[]{:S(2)}) async-start(bf16[16,8,1024]{2,1,0:T(8,128)(2,1)} %bitcast.14), calls=%async_computation.9 | async-start | bytes 524288 | tf_op jit(solution)/shard_map/all_to_all | solution.py:38
  263.2 0.1 reduce_sum.190
  263.3 11.3 %all-to-all-done.9 = bf16[16,8,1024]{2,1,0:T(8,128)(2,1)S(1)} async-done(((bf16[16,8,1024]{2,1,0:T(8,128)(2,1)}), bf16[16,8,1024]{2,1,0:T(8,128)(2,1)S(1)}, u32[]{:S(2)}, u32[]{:S(2)}) %all-to-all-start.9) | async-done | bytes 262176 | tf_op jit(solution)/shard_map/all_to_all | solution.py:38
  274.6 0.8 broadcast_in_dim.38
  275.4 3.5 %all-to-all-start.6 = ((bf16[16,4,2048]{2,1,0:T(4,128)(2,1)}), bf16[16,4,2048]{2,1,0:T(4,128)(2,1)S(1)}, u32[]{:S(2)}, u32[]{:S(2)}) async-start(bf16[16,4,2048]{2,1,0:T(4,128)(2,1)} %broadcast_in_dim.38), calls=%async_computation.6 | async-start | bytes 524288 | tf_op jit(solution)/shard_map/all_to_all | solution.py:16
  279.0 11.4 %all-to-all-done.6 = bf16[16,4,2048]{2,1,0:T(4,128)(2,1)S(1)} async-done(((bf16[16,4,2048]{2,1,0:T(4,128)(2,1)}), bf16[16,4,2048]{2,1,0:T(4,128)(2,1)S(1)}, u32[]{:S(2)}, u32[]{:S(2)}) %all-to-all-start.6) | async-done | bytes 262176 | tf_op jit(solution)/shard_map/all_to_all | solution.py:16
  290.4 0.7 broadcast_in_dim.39
  291.1 3.5 %all-to-all-start.10 = ((bf16[16,8,1024]{2,1,0:T(8,128)(2,1)}), bf16[16,8,1024]{2,1,0:T(8,128)(2,1)S(1)}, u32[]{:S(2)}, u32[]{:S(2)}) async-start(bf16[16,8,1024]{2,1,0:T(8,128)(2,1)} %broadcast_in_dim.39), calls=%async_computation.10 | async-start | bytes 524288 | tf_op jit(solution)/shard_map/all_to_all | solution.py:16
  294.6 0.8 reduce_sum.187
  295.4 0.6 fusion.42
  296.0 0.6 reduce_sum.200
  296.7 0.8 reshape.73
  297.5 8.5 %all-to-all-done.10 = bf16[16,8,1024]{2,1,0:T(8,128)(2,1)S(1)} async-done(((bf16[16,8,1024]{2,1,0:T(8,128)(2,1)}), bf16[16,8,1024]{2,1,0:T(8,128)(2,1)S(1)}, u32[]{:S(2)}, u32[]{:S(2)}) %all-to-all-start.10) | async-done | bytes 262176 | tf_op jit(solution)/shard_map/all_to_all | solution.py:16
  306.0 0.8 bitcast_convert_fusion
  (24 shorter events, 0.1 us)
Async XLA Ops:
  7.2 59.9 %all-gather.2.cloned.1.call-start = ((), (), s32[]{:S(2)}) async-start(), calls=%async_computation.13 | async-start | bytes 4456448 | tf_op jit(solution)/shard_map/all_gather | solution.py:109
  7.9 8.5 %copy-start.1 = (bf16[394,1024]{1,0:T(8,128)(2,1)S(1)}, bf16[394,1024]{1,0:T(8,128)(2,1)}, u32[]{:S(2)}) copy-start(bf16[394,1024]{1,0:T(8,128)(2,1)} %param.9) | copy-start | bytes 2420740
  10.5 33.0 %all-to-all-start = ((bf16[8,128,1024]{2,1,0:T(8,128)(2,1)}), bf16[8,128,1024]{2,1,0:T(8,128)(2,1)S(1)}, u32[]{:S(2)}, u32[]{:S(2)}) async-start(bf16[8,128,1024]{2,1,0:T(8,128)(2,1)} %broadcast_in_dim.36), calls=%async_computation | async-start | bytes 4194304 | tf_op jit(solution)/shard_map/all_to_all | solution.py:16
  52.8 14.2 %copy-start.4 = (f32[1,1024]{1,0:T(1,128)S(1)}, f32[1,1024]{1,0:T(1,128)}, u32[]{:S(2)}) copy-start(f32[1,1024]{1,0:T(1,128)} %param.13) | copy-start | bytes 12292
  52.8 14.2 %copy-start.5 = (f32[1024]{0:T(1024)S(1)}, f32[1024]{0:T(1024)}, u32[]{:S(2)}) copy-start(f32[1024]{0:T(1024)} %param.10) | copy-start | bytes 12292
  67.1 4.4 %copy-start.2 = (bf16[2,8,128,1024]{3,2,0,1:T(8,128)(2,1)S(1)}, bf16[2,8,128,1024]{3,2,0,1:T(8,128)(2,1)}, u32[]{:S(2)}) copy-start(bf16[2,8,128,1024]{3,2,0,1:T(8,128)(2,1)} %copy.27) | copy-start | bytes 12582916
  67.1 4.4 %copy-start.3 = (bf16[1,394,1024]{2,1,0:T(8,128)(2,1)S(1)}, bf16[1,394,1024]{2,1,0:T(8,128)(2,1)}, u32[]{:S(2)}) copy-start(bf16[1,394,1024]{2,1,0:T(8,128)(2,1)} %param.17) | copy-start | bytes 2420740
  67.1 4.4 %copy-start.7 = (f32[1,2048]{1,0:T(1,128)S(1)}, f32[1,2048]{1,0:T(1,128)}, u32[]{:S(2)}) copy-start(f32[1,2048]{1,0:T(1,128)} %param.14) | copy-start | bytes 24580
  67.1 4.4 %copy-start.8 = (f32[1,2048]{1,0:T(1,128)S(1)}, f32[1,2048]{1,0:T(1,128)}, u32[]{:S(2)}) copy-start(f32[1,2048]{1,0:T(1,128)} %param.15) | copy-start | bytes 24580
  71.5 2.4 copy-start.9
  83.1 4.6 %copy-start.6 = (bf16[1024,2048]{1,0:T(8,128)(2,1)S(1)}, bf16[1024,2048]{1,0:T(8,128)(2,1)}, u32[]{:S(2)}) copy-start(bf16[1024,2048]{1,0:T(8,128)(2,1)} %all-gather.2.cloned.1.call-done) | copy-start | bytes 12582916
  95.1 10.7 %all-to-all-start.3 = ((bf16[2,8,64,2048]{3,2,1,0:T(8,128)(2,1)}), bf16[2,8,64,2048]{3,2,1,0:T(8,128)(2,1)}, u32[]{:S(2)}, u32[]{:S(2)}) async-start(bf16[2,8,64,2048]{3,2,1,0:T(8,128)(2,1)} %bitcast.50), calls=%async_computation.3 | async-start | bytes 8388608 | tf_op jit(solution)/shard_map/all_to_all | solution.py:38
  118.3 27.1 %all-to-all-start.11 = ((f32[16,1,7168]{2,1,0:T(1,128)}), f32[16,1,7168]{2,1,0:T(1,128)S(1)}, u32[]{:S(2)}, u32[]{:S(2)}) async-start(f32[16,1,7168]{2,1,0:T(1,128)} %broadcast_in_dim.40), calls=%async_computation.11 | async-start | bytes 917504 | tf_op jit(solution)/shard_map/all_to_all | solution.py:16
  145.4 21.9 %all-to-all-start.2 = ((bf16[16,394,64]{1,2,0:T(8,128)(2,1)}), bf16[16,394,64]{1,2,0:T(8,128)(2,1)S(1)}, u32[]{:S(2)}, u32[]{:S(2)}) async-start(bf16[16,394,64]{1,2,0:T(8,128)(2,1)} %bitcast.9), calls=%async_computation.2 | async-start | bytes 2097152 | tf_op jit(solution)/shard_map/all_to_all | solution.py:38
  168.0 10.0 %all-to-all-start.12 = ((f32[16,1,1024]{2,1,0:T(1,128)}), f32[16,1,1024]{2,1,0:T(1,128)S(1)}, u32[]{:S(2)}, u32[]{:S(2)}) async-start(f32[16,1,1024]{2,1,0:T(1,128)} %broadcast_in_dim.45), calls=%async_computation.12 | async-start | bytes 131072 | tf_op jit(solution)/shard_map/all_to_all | solution.py:16
  177.9 31.5 %all-to-all-start.4 = ((bf16[8,64,2048]{2,1,0:T(8,128)(2,1)}), bf16[8,64,2048]{2,1,0:T(8,128)(2,1)S(1)}, u32[]{:S(2)}, u32[]{:S(2)}) async-start(bf16[8,64,2048]{2,1,0:T(8,128)(2,1)} %reduce_sum.188), calls=%async_computation.4 | async-start | bytes 4194304 | tf_op jit(solution)/shard_map/all_to_all | solution.py:46
  209.4 1.3 copy-start
  210.7 33.2 %all-to-all-start.8 = ((bf16[8,128,1024]{2,1,0:T(8,128)(2,1)}), bf16[8,128,1024]{2,1,0:T(8,128)(2,1)S(1)}, u32[]{:S(2)}, u32[]{:S(2)}) async-start(bf16[8,128,1024]{2,1,0:T(8,128)(2,1)} %reduce_sum.191), calls=%async_computation.8 | async-start | bytes 4194304 | tf_op jit(solution)/shard_map/all_to_all | solution.py:46
  243.9 15.7 %all-to-all-start.5 = ((bf16[16,4,2048]{2,1,0:T(4,128)(2,1)}), bf16[16,4,2048]{2,1,0:T(4,128)(2,1)S(1)}, u32[]{:S(2)}, u32[]{:S(2)}) async-start(bf16[16,4,2048]{2,1,0:T(4,128)(2,1)} %reshape.70), calls=%async_computation.5 | async-start | bytes 524288 | tf_op jit(solution)/shard_map/all_to_all | solution.py:38
  259.7 14.9 %all-to-all-start.9 = ((bf16[16,8,1024]{2,1,0:T(8,128)(2,1)}), bf16[16,8,1024]{2,1,0:T(8,128)(2,1)S(1)}, u32[]{:S(2)}, u32[]{:S(2)}) async-start(bf16[16,8,1024]{2,1,0:T(8,128)(2,1)} %bitcast.14), calls=%async_computation.9 | async-start | bytes 524288 | tf_op jit(solution)/shard_map/all_to_all | solution.py:38
  275.4 14.9 %all-to-all-start.6 = ((bf16[16,4,2048]{2,1,0:T(4,128)(2,1)}), bf16[16,4,2048]{2,1,0:T(4,128)(2,1)S(1)}, u32[]{:S(2)}, u32[]{:S(2)}) async-start(bf16[16,4,2048]{2,1,0:T(4,128)(2,1)} %broadcast_in_dim.38), calls=%async_computation.6 | async-start | bytes 524288 | tf_op jit(solution)/shard_map/all_to_all | solution.py:16
  291.1 14.9 %all-to-all-start.10 = ((bf16[16,8,1024]{2,1,0:T(8,128)(2,1)}), bf16[16,8,1024]{2,1,0:T(8,128)(2,1)S(1)}, u32[]{:S(2)}, u32[]{:S(2)}) async-start(bf16[16,8,1024]{2,1,0:T(8,128)(2,1)} %broadcast_in_dim.39), calls=%async_computation.10 | async-start | bytes 524288 | tf_op jit(solution)/shard_map/all_to_all | solution.py:16
Sparse Core Ops, SparseCore 0:
  9.8 57.1 all-gather.1
where the time goes:
time: 319 us; the launch traced here: 314 us
  waiting for transfers between devices  156 us (49%)
  starting transfers between devices  57.5 us (18%)
  matrix products  25.6 us (8%)
  local copies, waits for them, and re-layouts  21.3 us (7%)
  blocking collectives  20.3 us (6%)
  other arithmetic  18.9 us (6%)
  between operations  14.3 us (4%)
    all_to_all x5, waiting for transfers between devices, sent_to_all(): return lax.all_to_all(copies, axis, split_axis=0, concat_axis=0, tiled=True)  59.8 us
    all_to_all x2, waiting for transfers between devices, summed_rows(): lax.all_to_all(nearer.astype(jnp.bfloat16), far, split_axis=0, concat_axi...  46.2 us
    all_to_all x4, waiting for transfers between devices, sent_and_summed(): lax.all_to_all(tiles, axis, split_axis=0, concat_axis=0, tiled=True)  37.4 us
    all_to_all x5, starting transfers between devices, sent_to_all(): return lax.all_to_all(copies, axis, split_axis=0, concat_axis=0, tiled=True)  27.9 us
    all_to_all x4, starting transfers between devices, sent_and_summed(): lax.all_to_all(tiles, axis, split_axis=0, concat_axis=0, tiled=True)  19 us
    all_gather x1, waiting for transfers between devices, body(): expand_full = lax.all_gather(expand, MEMBER, axis=0, tiled=True)  11.8 us
    all_to_all x1, blocking collectives, sent_and_summed(): lax.all_to_all(tiles, axis, split_axis=0, concat_axis=0, tiled=True)  11.5 us
    reduce_sum x5, other arithmetic, sent_and_summed(): return arrived.astype(jnp.float32).sum(axis=0)  11.4 us
  transfers between devices with their start and end apart: 12, of which 11 were waited for; matrix products, arithmetic and copies ran while one was open for 10% of the time, Pallas kernels for 0%

commit v1 on v0

v1 whole, which is shorter than its diff:
```python
import functools

import jax
import jax.numpy as jnp
from jax import lax
from jax.experimental import pallas as pl
from jax.experimental.pallas import tpu as pltpu
from jax.sharding import Mesh
from jax.sharding import PartitionSpec as P

AXES = ("y", "x", "c", "z", "h")
MEMBER = ("y", "x", "c")
DP = ("z", "h")
TOK = 394
ROWS = 400
CUT = 208
FULL = 416
D = 1024
FF = 2048
SL = 512

eps = 1e-06
coeff = 0.7978845608028654
f32 = jnp.float32
bf16 = jnp.bfloat16
MESH = pl.DeviceIdType.MESH


def remote(src, dst, send, recv, **where):
    return pltpu.make_async_remote_copy(
        src_ref=src, dst_ref=dst, send_sem=send, recv_sem=recv, device_id=where, device_id_type=MESH
    )


def greet(barrier, **where):
    pl.semaphore_signal(barrier, inc=1, device_id=where, device_id_type=MESH)


def gelu_pair(hidden):
    inner = coeff * (hidden + 0.044715 * hidden * hidden * hidden)
    tangent = jnp.tanh(inner)
    active = 0.5 * hidden * (1.0 + tangent)
    slope = 0.5 * (1.0 + tangent) + 0.5 * hidden * (1.0 - tangent * tangent) * coeff * (
        1.0 + 3.0 * 0.044715 * hidden * hidden
    )
    return active, slope


def dot(a, b, ca, cb):
    return lax.dot_general(a, b, (((ca,), (cb,)), ((), ())), preferred_element_type=f32)


def row(v, i):
    return jnp.concatenate([v[i : i + 1], v[i + 1 : i + 2]], axis=1)


def compute_kernel(
    trunk, gain, vec, exp, shr, cot,
    ps, pe, t, sv, gp,
    normed, gained, invs, cots, w1, w2, vecs, si, act, pa, actf, proj, total, sacc, eacc,
    cs, cr, ws, wr, vs, vr, ss, sr, es, er,
):
    y, x, c = (lax.axis_index(a) for a in ("y", "x", "c"))
    xs = [lax.rem(x + o, 4) for o in range(4)]
    oy, oc = 1 - y, 1 - c
    barrier = pltpu.get_barrier_semaphore()
    for o in (1, 2, 3):
        greet(barrier, x=xs[o])
    greet(barrier, y=oy)
    greet(barrier, c=oc)
    pl.semaphore_wait(barrier, 5)

    slot_of = {1: 1, 3: 2, 2: 3}
    vec_copies, exp_copies = {}, {}
    for o in (1, 3, 2):
        vec_copies[o] = remote(
            vec.at[xs[o]], vecs.at[slot_of[o]], vs.at[o - 1], vr.at[o - 1], x=xs[o]
        )
        vec_copies[o].start()
        for half in (0, 1):
            exp_copies[o, half] = remote(
                exp.at[:, pl.ds(pl.multiple_of(1024 * half + 256 * xs[o], 256), 256)],
                w1.at[y, x, c, :, pl.ds(256 * half, 256)],
                ws.at[o - 1, half], wr.at[o - 1, half], x=xs[o],
            )
            exp_copies[o, half].start()
    shr_y = remote(shr, w2.at[y, c], ss.at[0], sr.at[0], y=oy)
    shr_c = remote(shr, w2.at[y, c], ss.at[1], sr.at[1], c=oc)
    shr_y.start()
    shr_c.start()
    a, b = pl.ds(0, CUT), pl.ds(CUT, ROWS - CUT)
    right_a = remote(cot.at[a], cots.at[1, a], cs.at[0], cr.at[1, 0], x=xs[1])
    left_b = remote(cot.at[b], cots.at[2, b], cs.at[2], cr.at[2, 1], x=xs[3])
    right_b = remote(cot.at[b], cots.at[1, b], cs.at[1], cr.at[1, 1], x=xs[1])
    left_a = remote(cot.at[a], cots.at[2, a], cs.at[3], cr.at[2, 0], x=xs[3])
    for copy in (right_a, left_b, right_b, left_a):
        copy.start()

    vecs[0] = vec[x]
    w2[y, c] = shr[...]
    for half in (0, 1):
        w1[y, x, c, :, 256 * half : 256 * half + 256] = exp[
            :, pl.ds(pl.multiple_of(1024 * half + 256 * x, 256), 256)
        ]
    cots[0] = cot[...]
    tokens = trunk[...].astype(f32)
    centered = tokens - jnp.mean(tokens, axis=1, keepdims=True)
    variance = jnp.mean(centered * centered, axis=1, keepdims=True)
    inv = lax.rsqrt(variance + eps)
    normed[...] = centered * inv
    gained[...] = centered * inv * gain[...]
    invs[...] = jnp.broadcast_to(inv, invs.shape)
    total[...] = jnp.zeros_like(total)
    sacc[...] = jnp.zeros_like(sacc)
    eacc[...] = jnp.zeros_like(eacc)

    for o in (1, 3, 2):
        exp_copies[o, 0].wait_recv()
        exp_copies[o, 1].wait_recv()
    exp_y = remote(w1.at[y, :, c], w1.at[y, :, c], es.at[0], er.at[0], y=oy)
    exp_c = remote(w1.at[y, :, c], w1.at[y, :, c], es.at[1], er.at[1], c=oc)
    exp_y.start()
    exp_c.start()
    shr_y.wait_recv()
    shr_f = remote(w2.at[oy, c], w2.at[oy, c], ss.at[2], sr.at[2], c=oc)
    shr_f.start()
    for o in (1, 3, 2):
        vec_copies[o].wait_recv()

    @pl.loop(0, 4)
    def _(k):
        si[k] = (gained[...] * row(vecs[k], 0)).astype(bf16)

    right_a.wait_recv()
    fwd_a = remote(cots.at[1, a], cots.at[3, a], cs.at[4], cr.at[3, 0], x=xs[1])
    fwd_a.start()
    left_b.wait_recv()
    fwd_b = remote(cots.at[2, b], cots.at[3, b], cs.at[5], cr.at[3, 1], x=xs[3])
    fwd_b.start()
    exp_y.wait_recv()
    exp_f = remote(w1.at[oy, :, c], w1.at[oy, :, c], es.at[2], er.at[2], c=oc)
    exp_f.start()
    for copy in (shr_c, exp_c, shr_f, exp_f):
        copy.wait_recv()

    @pl.loop(0, 4)
    def _(k):
        v = vecs[k]
        project = dot(si[k], w1[...].reshape(D, SL), 1, 0)
        active, slope = gelu_pair(project * v[4:5])
        proj[k] = project
        actf[k] = active
        act[k] = (active * v[5:6]).astype(bf16)
        pa[k] = slope * v[5:6]

    @pl.loop(0, 4)
    def _(k):
        @pl.when(k == 1)
        def _():
            right_b.wait_recv()

        @pl.when(k == 2)
        def _():
            left_a.wait_recv()

        @pl.when(k == 3)
        def _():
            fwd_a.wait_recv()
            fwd_b.wait_recv()

        v = vecs[k]
        scale_in, scale_out = row(v, 0), row(v, 2)
        first = w1[...].reshape(D, SL)
        second = w2[...].reshape(SL, D)
        seed = cots[k]
        scaled_cot = (seed.astype(f32) * scale_out).astype(bf16)
        back = dot(scaled_cot, second, 1, 1)
        grad_act = jnp.sum(back * actf[k], axis=0, keepdims=True)
        back_hidden = back * pa[k]
        grad_hid = jnp.sum(back_hidden * proj[k], axis=0, keepdims=True)
        back_proj = (back_hidden * v[4:5]).astype(bf16)
        both = dot(act[k], seed, 0, 0)
        sacc[...] += both * scale_out
        grad_out = jnp.sum(second.astype(f32) * both, axis=0, keepdims=True)
        back_norm = dot(back_proj, first, 1, 1)
        grad_in = jnp.sum(back_norm * gained[...], axis=0, keepdims=True)
        total[...] += back_norm * scale_in
        eacc[...] += dot(si[k], back_proj, 0, 0)
        zero = jnp.zeros((1, SL), f32)
        sv[k] = jnp.concatenate(
            [grad_in[:, :SL], grad_in[:, SL:], grad_out[:, :SL], grad_out[:, SL:], grad_hid, grad_act, zero, zero],
            axis=0,
        )

    whole = total[...]
    gp[...] = jnp.sum(whole * normed[...], axis=0, keepdims=True)
    unit = whole * gain[...]
    inner = jnp.mean(unit * normed[...], axis=1, keepdims=True)
    back_trunk = invs[:, :1] * (unit - jnp.mean(unit, axis=1, keepdims=True) - normed[...] * inner)
    term = (cot[...].astype(f32) + back_trunk).astype(bf16)
    t[0] = term[:CUT]
    t[1, : ROWS - CUT] = term[CUT:]
    t[1, ROWS - CUT :] = jnp.zeros((FULL - ROWS, D), bf16)
    for yy in (0, 1):
        for cc in (0, 1):
            ps[cc, yy] = sacc[(yy * 2 + cc) * 128 : (yy * 2 + cc + 1) * 128].astype(bf16)
            for xx in range(4):
                at = ((yy * 4 + xx) * 2 + cc) * 64
                pe[cc, yy, xx] = eacc[at : at + 64].astype(bf16)

    for copy in (right_a, left_b, right_b, left_a, fwd_a, fwd_b, shr_y, shr_c, shr_f, exp_y, exp_c, exp_f):
        copy.wait_send()
    for o in (1, 2, 3):
        vec_copies[o].wait_send()
        exp_copies[o, 0].wait_send()
        exp_copies[o, 1].wait_send()


def reduce_kernel(
    ps, pe, t, sv, gp,
    tg, eg, sg, ing, hg, ag, og, gg,
    rps, rpe, rt, qs, qe, tq, tr, rs, re, r16, rr, res, sh, ex, svr, gpr, dv, dvr, dvo, dvs, tf,
    as_, ar, bs, br, gs, gr, ys, yr, ts, tr_, rss, rrr, ds, dr, fs, fr, hs, hr, xs_, xr, os_, or_,
):
    y, x, c, z, h = (lax.axis_index(a) for a in AXES)
    oy, oc = 1 - y, 1 - c
    me = z * 2 + h
    chip = y * 4 + x
    barrier = pltpu.get_barrier_semaphore()

    @pl.loop(1, 64)
    def _(o):
        e = lax.rem(me + lax.rem(o, 16), 16)
        greet(barrier, x=lax.rem(x + o // 16, 4), z=e // 2, h=lax.rem(e, 2))

    for yo, co in ((0, 1), (1, 0), (1, 1)):
        for xo in range(4):
            greet(barrier, y=oy if yo else y, x=lax.rem(x + xo, 4), c=oc if co else c)
    pl.semaphore_wait(barrier, 75)

    sib = [
        remote(ps.at[oc], rps, as_.at[0], ar.at[0], c=oc),
        remote(pe.at[oc], rpe, as_.at[1], ar.at[1], c=oc),
        remote(t.at[oc], rt, as_.at[2], ar.at[2], c=oc),
    ]
    for copy in sib:
        copy.start()
    vecs = []
    for slot, xo in ((1, 3), (2, 1), (3, 2)):
        copy = remote(sv.at[slot], svr.at[x], bs.at[xo - 1], br.at[xo - 1], x=lax.rem(x + xo, 4))
        copy.start()
        vecs.append(copy)
    gains = []
    for o in range(1, 16):
        yo, xo, co = o // 8, (o // 2) % 4, o % 2
        copy = remote(
            gp, gpr.at[chip * 2 + c], gs.at[o], gr.at[o],
            y=oy if yo else y, x=lax.rem(x + xo, 4), c=oc if co else c,
        )
        gains.append(copy)
    svr[x] = sv[0]
    gpr[chip * 2 + c] = gp[...]

    sib[0].wait_recv()
    qs[...] = (ps[c].astype(f32) + rps[...].astype(f32)).astype(bf16)
    shrink_y = remote(qs.at[oy], rs, ys.at[0], yr.at[0], y=oy)
    shrink_y.start()
    sib[1].wait_recv()
    qe[...] = (pe[c].astype(f32) + rpe[...].astype(f32)).astype(bf16)
    expand_y = remote(qe.at[oy], re, ys.at[1], yr.at[1], y=oy)
    expand_y.start()
    sib[2].wait_recv()
    joint = (t[c].astype(f32) + rt[...].astype(f32)).astype(bf16)
    for g in range(8):
        tq[g] = joint[:, 128 * g : 128 * g + 128]
    tiles = []
    for g in range(1, 8):
        yo, xo = g // 4, g % 4
        ty, tx = oy if yo else y, lax.rem(x + xo, 4)
        copy = remote(tq.at[ty * 4 + tx], tr.at[chip], ts.at[g], tr_.at[g], y=ty, x=tx)
        copy.start()
        tiles.append(copy)
    for copy in gains:
        copy.start()
    tr[chip] = tq[chip]

    for copy in vecs:
        copy.wait_recv()
    for copy in gains:
        copy.wait_recv()
    sums = svr[0] + svr[1] + svr[2] + svr[3]
    gain_sum = gpr[0]
    for m in range(1, 16):
        gain_sum = gain_sum + gpr[m]
    zero = jnp.zeros((1, SL), f32)
    for i in range(4):
        dv[i] = sums[i : i + 1]
        dv[4 + i] = svr[i, 4:5]
        dv[8 + i] = svr[i, 5:6]
    dv[12] = gain_sum[:, :SL]
    dv[13] = gain_sum[:, SL:]
    dv[14] = zero
    dv[15] = zero

    peers = []
    for o in range(1, 16):
        e = lax.rem(me + o, 16)
        peers.append((o, e, e // 2, lax.rem(e, 2)))
    small = []
    for o, e, ez, eh in peers:
        copy = remote(dv.at[e], dvr.at[me], ds.at[o], dr.at[o], z=ez, h=eh)
        copy.start()
        small.append(copy)
    dvr[me] = dv[me]

    shrink_y.wait_recv()
    mine = (qs[y].astype(f32) + rs[...].astype(f32)).astype(bf16)
    for p in range(16):
        r16[p, :, :SL] = mine[16 * (p // 2) : 16 * (p // 2) + 16, SL * (p % 2) : SL * (p % 2) + SL]
    expand_y.wait_recv()
    mine = (qe[y].astype(f32) + re[...].astype(f32)).astype(bf16)
    for p in range(16):
        r16[p, :, SL:] = mine[p // 4, 16 * (p % 4) : 16 * (p % 4) + 16]
    parts = []
    for o, e, ez, eh in peers:
        copy = remote(r16.at[e], rr.at[me], rss.at[o], rrr.at[o], z=ez, h=eh)
        copy.start()
        parts.append(copy)
    rr[me] = r16[me]

    for copy in tiles:
        copy.wait_recv()
    summed = tr[0].astype(f32)
    for g in range(1, 8):
        summed = summed + tr[g].astype(f32)
    tf[c] = summed.astype(bf16)
    finish = remote(tf.at[c], tf.at[c], fs, fr, c=oc)
    finish.start()

    for copy in small:
        copy.wait_recv()
    line = dvr[0]
    for p in range(1, 16):
        line = line + dvr[p]
    dvs[...] = line
    back = []
    for o, e, ez, eh in peers:
        copy = remote(dvs, dvo.at[me], os_.at[o], or_.at[o], z=ez, h=eh)
        copy.start()
        back.append(copy)
    dvo[me] = line

    for copy in parts:
        copy.wait_recv()
    done = rr[0].astype(f32)
    for p in range(1, 16):
        done = done + rr[p].astype(f32)
    done = done.astype(bf16)
    res[0] = done[:, :SL]
    res[1] = done[:, SL:]
    goal = me // 4
    spread, shrinks = [], []
    for o, e, ez, eh in peers:
        copy = remote(res.at[1], ex.at[x, lax.rem(me, 4)], xs_.at[o], xr.at[x, lax.rem(me, 4)], x=goal, z=ez, h=eh)
        copy.start()
        spread.append(copy)
        copy = remote(res.at[0], sh.at[me], hs.at[o], hr.at[o], z=ez, h=eh)
        copy.start()
        shrinks.append(copy)
    own = remote(res.at[1], ex.at[x, lax.rem(me, 4)], xs_.at[0], xr.at[x, lax.rem(me, 4)], x=goal)

    @pl.when(goal != x)
    def _():
        own.start()

    @pl.when(goal == x)
    def _():
        ex[x, lax.rem(me, 4)] = done[:, SL:]

    sh[me] = done[:, :SL]

    finish.wait_recv()
    low = tf[0].astype(f32)
    high = tf[1].astype(f32)
    tg[:CUT] = jnp.where(c == 0, low[:, :64], low[:, 64:]).astype(bf16)
    tg[CUT:] = jnp.where(c == 0, high[: TOK - CUT, :64], high[: TOK - CUT, 64:]).astype(bf16)
    for copy in back:
        copy.wait_recv()
    for i in (0, 1):
        ing[:, SL * i : SL * i + SL] = dvo[i]
        og[:, SL * i : SL * i + SL] = dvo[2 + i]
        gg[:, SL * i : SL * i + SL] = dvo[12 + i]
        for xx in range(4):
            at = 1024 * i + 256 * xx
            hg[:, at : at + 256] = dvo[4 + xx][:, 256 * i : 256 * i + 256]
            ag[:, at : at + 256] = dvo[8 + xx][:, 256 * i : 256 * i + 256]
    for copy in shrinks:
        copy.wait_recv()
    for p in range(16):
        sg[16 * (p // 2) : 16 * (p // 2) + 16, SL * (p % 2) : SL * (p % 2) + SL] = sh[p].astype(f32)
    for xx in range(4):
        for q in range(4):

            @pl.when(jnp.logical_or(x != xx, me != 4 * x + q))
            def _():
                remote(res.at[1], ex.at[xx, q], xs_.at[0], xr.at[xx, q], x=goal).wait_recv()

            for i in (0, 1):
                at = 1024 * i + 256 * xx
                eg[16 * q : 16 * q + 16, at : at + 256] = ex[xx, q, :, 256 * i : 256 * i + 256].astype(f32)

    for copy in sib + vecs + gains + [shrink_y, expand_y] + tiles + small + parts + [finish] + back + spread + shrinks:
        copy.wait_send()

    @pl.when(goal != x)
    def _():
        own.wait_send()


def vmem(n):
    return [pl.BlockSpec(memory_space=pltpu.VMEM)] * n


def dma(*shape):
    return pltpu.SemaphoreType.DMA(shape)


def body(trunk, normgain, expand, shrink, inscale, hidscale, actscale, outscale, cotangent):
    S = jax.ShapeDtypeStruct
    pad = ((0, ROWS - TOK), (0, 0))

    def sliced(v):
        return v.reshape(2, 4, 256).swapaxes(0, 1).reshape(4, 1, SL)

    def twice(v):
        return jnp.broadcast_to(v.reshape(1, 2, SL), (4, 2, SL))

    vec = jnp.concatenate(
        [twice(inscale), twice(outscale), sliced(hidscale), sliced(actscale), jnp.zeros((4, 2, SL), f32)], axis=1
    )
    ps, pe, t, sv, gp = pl.pallas_call(
        compute_kernel,
        out_shape=[
            S((2, 2, 128, D), bf16),
            S((2, 2, 4, 64, SL), bf16),
            S((2, CUT, D), bf16),
            S((4, 8, SL), f32),
            S((1, D), f32),
        ],
        in_specs=vmem(6),
        out_specs=vmem(5),
        scratch_shapes=[
            pltpu.VMEM((ROWS, D), f32),
            pltpu.VMEM((ROWS, D), f32),
            pltpu.VMEM((ROWS, 128), f32),
            pltpu.VMEM((4, ROWS, D), bf16),
            pltpu.VMEM((2, 4, 2, 64, SL), bf16),
            pltpu.VMEM((2, 2, 128, D), bf16),
            pltpu.VMEM((4, 8, SL), f32),
            pltpu.VMEM((4, ROWS, D), bf16),
            pltpu.VMEM((4, ROWS, SL), bf16),
            pltpu.VMEM((4, ROWS, SL), f32),
            pltpu.VMEM((4, ROWS, SL), f32),
            pltpu.VMEM((4, ROWS, SL), f32),
            pltpu.VMEM((ROWS, D), f32),
            pltpu.VMEM((SL, D), f32),
            pltpu.VMEM((D, SL), f32),
            dma(6), dma(4, 2), dma(3, 2), dma(3, 2), dma(3), dma(3), dma(3), dma(3), dma(3), dma(3),
        ],
        compiler_params=pltpu.CompilerParams(
            collective_id=0, has_side_effects=True, vmem_limit_bytes=60 * 1024 * 1024
        ),
        name="gather_compute",
    )(
        jnp.pad(trunk, pad), normgain.reshape(1, D), vec, expand, shrink, jnp.pad(cotangent[0], pad)
    )
    tg, eg, sg, ing, hg, ag, og, gg = pl.pallas_call(
        reduce_kernel,
        out_shape=[
            S((TOK, 64), bf16),
            S((64, FF), f32),
            S((128, D), f32),
            S((1, D), f32),
            S((1, FF), f32),
            S((1, FF), f32),
            S((1, D), f32),
            S((1, D), f32),
        ],
        in_specs=vmem(5),
        out_specs=vmem(8),
        scratch_shapes=[
            pltpu.VMEM((2, 128, D), bf16),
            pltpu.VMEM((2, 4, 64, SL), bf16),
            pltpu.VMEM((CUT, D), bf16),
            pltpu.VMEM((2, 128, D), bf16),
            pltpu.VMEM((2, 4, 64, SL), bf16),
            pltpu.VMEM((8, CUT, 128), bf16),
            pltpu.VMEM((8, CUT, 128), bf16),
            pltpu.VMEM((128, D), bf16),
            pltpu.VMEM((4, 64, SL), bf16),
            pltpu.VMEM((16, 16, D), bf16),
            pltpu.VMEM((16, 16, D), bf16),
            pltpu.VMEM((2, 16, SL), bf16),
            pltpu.VMEM((16, 16, SL), bf16),
            pltpu.VMEM((4, 4, 16, SL), bf16),
            pltpu.VMEM((4, 8, SL), f32),
            pltpu.VMEM((16, 1, D), f32),
            pltpu.VMEM((16, 1, SL), f32),
            pltpu.VMEM((16, 1, SL), f32),
            pltpu.VMEM((16, 1, SL), f32),
            pltpu.VMEM((1, SL), f32),
            pltpu.VMEM((2, CUT, 128), bf16),
            dma(3), dma(3), dma(3), dma(3), dma(16), dma(16), dma(2), dma(2), dma(8), dma(8),
            dma(16), dma(16), dma(16), dma(16), pltpu.SemaphoreType.DMA, pltpu.SemaphoreType.DMA,
            dma(16), dma(16), dma(16), dma(4, 4), dma(16), dma(16),
        ],
        compiler_params=pltpu.CompilerParams(
            collective_id=1, has_side_effects=True, vmem_limit_bytes=40 * 1024 * 1024
        ),
        name="reduce",
    )(ps, pe, t, sv, gp)
    return tg, eg, sg, ing, hg, ag, og, gg.reshape(D)


def solution(mesh):
    finer = Mesh(mesh.devices.reshape(2, 4, 2, 8, 2), AXES)
    rows = P(MEMBER, None)
    in_specs = (P(DP, None), P(), rows, rows, rows, rows, rows, rows, P(MEMBER, DP, None))
    out_specs = (P(DP, MEMBER), rows, rows, rows, rows, rows, rows, P())
    return jax.shard_map(body, mesh=finer, in_specs=in_specs, out_specs=out_specs, check_vma=False)
```

time: 319 us -> 125 us (0.39); the launches traced: 314 us -> 124 us
  waiting for transfers between devices: 156 us -> 0 us
  Pallas kernels: 0 us -> 104 us
  starting transfers between devices: 57.5 us -> 0 us
  matrix products: 25.6 us -> 0 us
  blocking collectives: 20.3 us -> 0 us
  other arithmetic: 18.9 us -> 2.67 us
  between operations: 14.3 us -> 0.79 us
  local copies, waits for them, and re-layouts: 21.3 us -> 16.4 us
    all_to_all x11 -> x0, waiting for transfers between devices: 143 us -> none  [the longest x5 59.8 us: sent_to_all(): return lax.all_to_all(copies, axis, split_axis=0, concat_axis=0, tiled=True)]
    pallas_call x0 -> x2, Pallas kernels: none -> 104 us  [the longest x1 61.9 us: body(): pl.pallas_call(reduce_kernel, out_shape=[S((TOK, 64), bf16), S((64, FF),...]
    all_to_all x11 -> x0, starting transfers between devices: 57.4 us -> none  [the longest x5 27.9 us: sent_to_all(): return lax.all_to_all(copies, axis, split_axis=0, concat_axis=0, tiled=True)]
    dot_general x6 -> x0, matrix products: 25.6 us -> none  [the longest x2 9.53 us: rounded_term(): lax.dot_general(left, right, (((0,), (0,)), ((), ())), preferred_element_...]
    all_to_all x2 -> x0, blocking collectives: 20.3 us -> none  [the longest x1 11.5 us: sent_and_summed(): lax.all_to_all(tiles, axis, split_axis=0, concat_axis=0, tiled=True)]
    reduce_sum x11 -> x0, other arithmetic: 15.9 us -> none  [the longest x5 11.4 us: sent_and_summed(): return arrived.astype(jnp.float32).sum(axis=0)]
    all_gather x1 -> x0, waiting for transfers between devices: 11.8 us -> none  [body(): expand_full = lax.all_gather(expand, MEMBER, axis=0, tiled=True)]
    unnamed x24 -> x29, local copies, waits for them, and re-layouts: 1.34 us -> 12.4 us
  transfers between devices with their start and end apart: 12 -> 0, of which waited for: 11 -> 0; matrix products, arithmetic and copies ran while one was open for 10% -> 0% of each run, Pallas kernels for 0% -> 0%
where the time goes in v1:
time: 125 us; the launch traced here: 124 us
  Pallas kernels  104 us (83%)
  local copies, waits for them, and re-layouts  16.4 us (13%)
  other arithmetic  2.67 us (2%)
    pallas_call x1, Pallas kernels, body(): pl.pallas_call(reduce_kernel, out_shape=[S((TOK, 64), bf16), S((64, FF),...  61.9 us
    pallas_call x1, Pallas kernels, body(): pl.pallas_call(compute_kernel, out_shape=[S((2, 2, 128, D), bf16), S((2,...  41.9 us
    unnamed x29, local copies, waits for them, and re-layouts  12.4 us
    unnamed x4, other arithmetic  2.67 us

profile of v1, /device:TPU:1, one launch (start us, length us, event | category | flops | bytes accessed | tf_op | source)
XLA Modules:
  0.0 123.6 jit_solution(9364317426671537666)
XLA Ops:
  0.6 0.0 copy-start.8
  0.6 0.5 broadcast.16
  1.2 0.2 copy-done.8
  1.3 0.7 reduce.13
  2.0 0.0 copy-start.9
  2.0 0.7 copy-done.9
  2.7 0.0 copy-start.6
  2.7 0.7 reduce.14
  3.4 0.0 copy-done.6
  3.4 0.7 reduce.15
  4.1 0.0 copy-start.7
  4.1 0.7 copy-done.7
  4.8 0.7 reduce.16
  5.6 0.7 concatenate.3.vec
  6.2 0.0 copy-start.5
  6.2 2.2 %pad.7.trunk = bf16[400,1024]{1,0:T(8,128)(2,1)} pad(bf16[394,1024]{1,0:T(8,128)(2,1)} %param.9, bf16[]{:T(256)} %constant.1.clone.1), padding=0_6x0_0 | pad | bytes 1626114 | tf_op jit(solution)/shard_map/jit(_pad)/pad | solution.py:475
  8.4 0.0 copy-done.5
  8.4 0.9 pad.8.cot
  9.4 41.9 %gather_compute.1 = (bf16[2,2,128,1024]{3,2,1,0:T(8,128)(2,1)}, bf16[2,2,4,64,512]{4,3,2,1,0:T(8,128)(2,1)}, bf16[2,208,1024]{2,1,0:T(8,128)(2,1)}, f32[4,8,512]{2,1,0:T(8,128)}, f32[1,1024]{1,0:T(1,128)}) custom-call(bf16[400,1024]{1,0:T(8,128)(2,1)} %pad.7.trunk, f32[1,1024]{1,0:T(1,128)} %bitcast.13, f32[4,8,512]{2,1,0:T(8,128)} %concatenate.3.vec, ...), custom_call_target="tpu_custom_call" | custom-call | tf_op jit(solution)/shard_map/gather_compute/pallas_call | solution.py:441
  51.3 0.0 copy-start.4
  51.3 0.7 copy-done.4
  51.9 0.0 copy-start
  51.9 1.2 copy-done
  53.2 0.0 copy-start.1
  53.2 1.2 copy-done.1
  54.4 0.0 copy-start.2
  54.4 1.2 copy-done.2
  55.6 0.0 copy-start.3
  55.6 0.8 copy-done.3
  56.4 61.9 %reduce.17 = (bf16[394,64]{1,0:T(8,128)(2,1)S(1)}, f32[64,2048]{1,0:T(8,128)S(1)}, f32[128,1024]{1,0:T(8,128)S(1)}, f32[1,1024]{1,0:T(1,128)S(1)}, f32[1,2048]{1...) custom-call(bf16[2,2,128,1024]{3,2,1,0:T(8,128)(2,1)S(1)} %copy-done, ...), custom_call_target="tpu_custom_call" | custom-call | tf_op jit(solution)/shard_map/reduce/pallas_call | solution.py:477
  118.3 0.7 copy.19
  119.0 0.8 copy.31
  119.8 0.8 copy.32
  120.6 0.6 copy.33
  121.2 0.6 copy.34
  121.8 0.6 copy.35
  122.4 0.6 copy.36
  123.0 0.6 copy.37
  (11 shorter events, 0.1 us)
Async XLA Ops:
  0.6 0.7 copy-start.8
  2.0 0.7 copy-start.9
  2.7 0.7 copy-start.6
  4.1 0.7 copy-start.7
  6.2 2.2 %copy-start.5 = (bf16[1,394,1024]{2,1,0:T(8,128)(2,1)S(1)}, bf16[1,394,1024]{2,1,0:T(8,128)(2,1)}, u32[]{:S(2)}) copy-start(bf16[1,394,1024]{2,1,0:T(8,128)(2,1)} %param.17) | copy-start | bytes 2420740
  51.3 0.7 copy-start.4
  51.9 1.2 copy-start
  53.2 1.2 copy-start.1
  54.4 1.2 copy-start.2
  55.6 0.8 copy-start.3

commit v2 on v1

v2 whole, which is shorter than its diff:
```python
import jax
import jax.numpy as jnp
from jax import lax
from jax.experimental import pallas as pl
from jax.experimental.pallas import tpu as pltpu
from jax.sharding import Mesh
from jax.sharding import PartitionSpec as P

AXES = ("y", "x", "c", "z", "h")
MEMBER = ("y", "x", "c")
DP = ("z", "h")
TOK = 394
CUT = 208
FULL = 416
D = 1024
FF = 2048
SL = 512

eps = 1e-06
coeff = 0.7978845608028654
f32 = jnp.float32
bf16 = jnp.bfloat16
MESH = pl.DeviceIdType.MESH


def remote(src, dst, send, recv, **where):
    return pltpu.make_async_remote_copy(
        src_ref=src, dst_ref=dst, send_sem=send, recv_sem=recv, device_id=where, device_id_type=MESH
    )


def greet(barrier, **where):
    pl.semaphore_signal(barrier, inc=1, device_id=where, device_id_type=MESH)


def gelu_pair(hidden):
    inner = coeff * (hidden + 0.044715 * hidden * hidden * hidden)
    tangent = jnp.tanh(inner)
    active = 0.5 * hidden * (1.0 + tangent)
    slope = 0.5 * (1.0 + tangent) + 0.5 * hidden * (1.0 - tangent * tangent) * coeff * (
        1.0 + 3.0 * 0.044715 * hidden * hidden
    )
    return active, slope


def dot(a, b, ca, cb):
    return lax.dot_general(a, b, (((ca,), (cb,)), ((), ())), preferred_element_type=f32)


def row(v, i):
    return jnp.concatenate([v[i : i + 1], v[i + 1 : i + 2]], axis=1)


def added(*refs):
    total = refs[0].astype(f32)
    for r in refs[1:]:
        total = total + r.astype(f32)
    return total


def kernel(
    trunk, exp, shr, cot, gain, inscale, hidscale, actscale, outscale,
    tf, sh, ex, dvo,
    tbuf, vec, normed, gained, invs, cots, w1, w2, vecs, si, act, pa, actf, proj, total, sacc, eacc,
    pbuf, rbuf, t, rt, q, yb, mix, r, rz, res, tq, tr, sv, svr, gp, gpr, dv, dvr, dvs,
    ls, cs, cr, ws, wr, vs, vr, ss, sr, es, er,
    as_, ar, ys, yr, zs, zr, hs, hr, xs_, xr, ts, tr_, fs, fr, bs, br, gs, gr, ds, dr, os_, or_,
):
    y, x, c, z, h = (lax.axis_index(a) for a in AXES)
    xs = [lax.rem(x + o, 4) for o in range(4)]
    oy, oc = 1 - y, 1 - c
    me = z * 2 + h
    chip = y * 4 + x
    place = h * 2 + y
    sent = []

    def go(copy):
        copy.start()
        sent.append(copy)
        return copy

    barrier = pltpu.get_barrier_semaphore()

    @pl.loop(1, 64)
    def _(o):
        e = lax.rem(me + lax.rem(o, 16), 16)
        greet(barrier, x=lax.rem(x + o // 16, 4), z=e // 2, h=lax.rem(e, 2))

    for yo, co in ((0, 1), (1, 0), (1, 1)):
        for xo in range(4):
            greet(barrier, y=oy if yo else y, x=xs[xo], c=oc if co else c)
    greet(barrier, y=oy, h=1 - h)

    here = [
        pltpu.make_async_copy(trunk, tbuf, ls.at[0]),
        pltpu.make_async_copy(shr, w2.at[y, c], ls.at[1]),
        pltpu.make_async_copy(cot.at[0], cots.at[0], ls.at[2]),
    ]
    for half in (0, 1):
        here.append(
            pltpu.make_async_copy(
                exp.at[:, pl.ds(pl.multiple_of(1024 * half + 256 * x, 256), 256)],
                w1.at[y, x, c, :, pl.ds(256 * half, 256)],
                ls.at[3 + half],
            )
        )
    for copy in here:
        copy.start()
    for xx in range(4):
        for i in (0, 1):
            vec[xx, i : i + 1] = inscale[:, SL * i : SL * i + SL]
            vec[xx, 2 + i : 3 + i] = outscale[:, SL * i : SL * i + SL]
            at = 1024 * i + 256 * xx
            vec[xx, 4:5, 256 * i : 256 * i + 256] = hidscale[:, at : at + 256]
            vec[xx, 5:6, 256 * i : 256 * i + 256] = actscale[:, at : at + 256]
        vec[xx, 6:8] = jnp.zeros((2, SL), f32)
    pl.semaphore_wait(barrier, 76)

    slot_of = {1: 1, 3: 2, 2: 3}
    vec_copies, exp_copies = {}, {}
    for o in (1, 3, 2):
        for half in (0, 1):
            exp_copies[o, half] = go(remote(
                exp.at[:, pl.ds(pl.multiple_of(1024 * half + 256 * xs[o], 256), 256)],
                w1.at[y, x, c, :, pl.ds(256 * half, 256)],
                ws.at[o - 1, half], wr.at[o - 1, half], x=xs[o],
            ))
        vec_copies[o] = go(remote(
            vec.at[xs[o]], vecs.at[slot_of[o]], vs.at[o - 1], vr.at[o - 1], x=xs[o]
        ))
    shr_y = go(remote(shr, w2.at[y, c], ss.at[0], sr.at[0], y=oy))
    shr_c = go(remote(shr, w2.at[y, c], ss.at[1], sr.at[1], c=oc))
    a, b = pl.ds(0, CUT), pl.ds(CUT, TOK - CUT)
    right_a = go(remote(cot.at[0, a], cots.at[1, a], cs.at[0], cr.at[1, 0], x=xs[1]))
    left_b = go(remote(cot.at[0, b], cots.at[2, b], cs.at[2], cr.at[2, 1], x=xs[3]))
    right_b = go(remote(cot.at[0, b], cots.at[1, b], cs.at[1], cr.at[1, 1], x=xs[1]))
    left_a = go(remote(cot.at[0, a], cots.at[2, a], cs.at[3], cr.at[2, 0], x=xs[3]))

    vecs[0] = vec[x]
    here[0].wait()
    tokens = tbuf[...].astype(f32)
    centered = tokens - jnp.mean(tokens, axis=1, keepdims=True)
    variance = jnp.mean(centered * centered, axis=1, keepdims=True)
    inv = lax.rsqrt(variance + eps)
    normed[...] = centered * inv
    gained[...] = centered * inv * gain[...]
    invs[...] = jnp.broadcast_to(inv, invs.shape)
    total[...] = jnp.zeros_like(total)
    sacc[...] = jnp.zeros_like(sacc)
    eacc[...] = jnp.zeros_like(eacc)
    for copy in here[1:]:
        copy.wait()

    for o in (1, 3, 2):
        exp_copies[o, 0].wait_recv()
        exp_copies[o, 1].wait_recv()
    exp_y = go(remote(w1.at[y, :, c], w1.at[y, :, c], es.at[0], er.at[0], y=oy))
    exp_c = go(remote(w1.at[y, :, c], w1.at[y, :, c], es.at[1], er.at[1], c=oc))
    shr_y.wait_recv()
    shr_f = go(remote(w2.at[oy, c], w2.at[oy, c], ss.at[2], sr.at[2], c=oc))
    for o in (1, 3, 2):
        vec_copies[o].wait_recv()

    @pl.loop(0, 4)
    def _(k):
        si[k] = (gained[...] * row(vecs[k], 0)).astype(bf16)

    right_a.wait_recv()
    fwd_a = go(remote(cots.at[1, a], cots.at[3, a], cs.at[4], cr.at[3, 0], x=xs[1]))
    left_b.wait_recv()
    fwd_b = go(remote(cots.at[2, b], cots.at[3, b], cs.at[5], cr.at[3, 1], x=xs[3]))
    exp_y.wait_recv()
    exp_f = go(remote(w1.at[oy, :, c], w1.at[oy, :, c], es.at[2], er.at[2], c=oc))
    for copy in (shr_c, exp_c, shr_f, exp_f):
        copy.wait_recv()

    @pl.loop(0, 4)
    def _(k):
        v = vecs[k]
        project = dot(si[k], w1[...].reshape(D, SL), 1, 0)
        active, slope = gelu_pair(project * v[4:5])
        proj[k] = project
        actf[k] = active
        act[k] = (active * v[5:6]).astype(bf16)
        pa[k] = slope * v[5:6]

    def back_part(k):
        v = vecs[k]
        scale_out = row(v, 2)
        second = w2[...].reshape(SL, D)
        seed = cots[k]
        scaled_cot = (seed.astype(f32) * scale_out).astype(bf16)
        back = dot(scaled_cot, second, 1, 1)
        grad_act = jnp.sum(back * actf[k], axis=0, keepdims=True)
        back_hidden = back * pa[k]
        grad_hid = jnp.sum(back_hidden * proj[k], axis=0, keepdims=True)
        back_proj = (back_hidden * v[4:5]).astype(bf16)
        both = dot(act[k], seed, 0, 0)
        sacc[...] += both * scale_out
        grad_out = jnp.sum(second.astype(f32) * both, axis=0, keepdims=True)
        zero = jnp.zeros((2, SL), f32)
        sv[k, 2:8] = jnp.concatenate([grad_out[:, :SL], grad_out[:, SL:], grad_hid, grad_act, zero], axis=0)
        return back_proj

    def expand_part(k, back_proj):
        eacc[...] += dot(si[k], back_proj, 0, 0)

    def norm_part(k, back_proj):
        back_norm = dot(back_proj, w1[...].reshape(D, SL), 1, 1)
        grad_in = jnp.sum(back_norm * gained[...], axis=0, keepdims=True)
        total[...] += back_norm * row(vecs[k], 0)
        sv[k, 0:2] = jnp.concatenate([grad_in[:, :SL], grad_in[:, SL:]], axis=0)

    @pl.loop(0, 3)
    def _(k):
        @pl.when(k == 1)
        def _():
            right_b.wait_recv()

        @pl.when(k == 2)
        def _():
            left_a.wait_recv()

        back_proj = back_part(k)
        expand_part(k, back_proj)
        norm_part(k, back_proj)

    right, left, far = (lax.rem(place + o, 4) for o in (1, 3, 2))
    to_right = dict(y=lax.rem(right, 2), h=right // 2)
    to_left = dict(y=lax.rem(left, 2), h=left // 2)
    top, low = pl.ds(0, 4), pl.ds(4, 4)

    def core_step(i):
        return go(remote(pbuf.at[i, oc], rbuf.at[i], as_.at[i], ar.at[i], c=oc))

    def ring_start(i, copy):
        copy.wait_recv()
        q[i] = added(pbuf[i, c], rbuf[i]).astype(bf16)
        return [
            go(remote(q.at[i, far, top], yb.at[i, 0], ys.at[i, 0], yr.at[i, 0], **to_right)),
            go(remote(q.at[i, far, low], yb.at[i, 1], ys.at[i, 1], yr.at[i, 1], **to_left)),
            go(remote(q.at[i, right, low], yb.at[i, 2], ys.at[i, 2], yr.at[i, 2], **to_right)),
            go(remote(q.at[i, left, top], yb.at[i, 3], ys.at[i, 3], yr.at[i, 3], **to_left)),
        ]

    def ring_pass(i, copies):
        copies[0].wait_recv()
        mix[i, 0] = added(q[i, right, 0:4], yb[i, 0]).astype(bf16)
        copies.append(go(remote(mix.at[i, 0], yb.at[i, 4], ys.at[i, 4], yr.at[i, 4], **to_right)))
        copies[1].wait_recv()
        mix[i, 1] = added(q[i, left, 4:8], yb[i, 1]).astype(bf16)
        copies.append(go(remote(mix.at[i, 1], yb.at[i, 5], ys.at[i, 5], yr.at[i, 5], **to_left)))

    def deep_start(i, copies):
        for copy in copies[2:]:
            copy.wait_recv()
        r[i, 0:4] = added(q[i, place, 0:4], yb[i, 3], yb[i, 4]).astype(bf16)
        r[i, 4:8] = added(q[i, place, 4:8], yb[i, 2], yb[i, 5]).astype(bf16)
        out = []
        for o in (4, 3, 5, 2, 6, 1, 7):
            e = lax.rem(z + o, 8)
            out.append(go(remote(r.at[i, e], rz.at[i, z], zs.at[i, o], zr.at[i, o], z=e)))
        rz[i, z] = r[i, z]
        return out

    def deep_sum(i, copies):
        for copy in copies:
            copy.wait_recv()
        done = added(*(rz[i, e] for e in range(8))).astype(bf16)
        res[i] = done
        return done

    peers = []
    for o in range(1, 16):
        e = lax.rem(me + o, 16)
        peers.append((o, dict(z=e // 2, h=lax.rem(e, 2))))

    fwd_a.wait_recv()
    fwd_b.wait_recv()
    back_proj = back_part(3)
    for cc in (0, 1):
        for hh in (0, 1):
            for yy in (0, 1):
                at = (yy * 2 + cc) * 128
                block = sacc[at : at + 128, SL * hh : SL * hh + SL]
                pbuf[0, cc, 2 * hh + yy] = block.astype(bf16).reshape(8, 16, SL)
    core_s = core_step(0)
    expand_part(3, back_proj)
    for cc in (0, 1):
        for hh in (0, 1):
            for yy in (0, 1):
                for zz in range(8):
                    at = ((yy * 4 + zz // 2) * 2 + cc) * 64 + zz % 2 * 32 + hh * 16
                    pbuf[1, cc, 2 * hh + yy, zz] = eacc[at : at + 16].astype(bf16)
    core_e = core_step(1)
    ring_s = ring_start(0, core_s)
    norm_part(3, back_proj)
    ring_e = ring_start(1, core_e)

    vector_copies = []
    for slot, xo in ((1, 3), (2, 1), (3, 2)):
        vector_copies.append(go(remote(sv.at[slot], svr.at[x], bs.at[xo - 1], br.at[xo - 1], x=xs[xo])))
    svr[x] = sv[0]
    whole = total[...]
    gp[...] = jnp.sum(whole * normed[...], axis=0, keepdims=True)
    gains = []
    for o in range(1, 16):
        yo, xo, co = o // 8, (o // 2) % 4, o % 2
        gains.append(go(remote(
            gp, gpr.at[chip * 2 + c], gs.at[o], gr.at[o], y=oy if yo else y, x=xs[xo], c=oc if co else c
        )))
    gpr[chip * 2 + c] = gp[...]
    unit = whole * gain[...]
    inner = jnp.mean(unit * normed[...], axis=1, keepdims=True)
    back_trunk = invs[:, :1] * (unit - jnp.mean(unit, axis=1, keepdims=True) - normed[...] * inner)
    term = (cots[0].astype(f32) + back_trunk).astype(bf16)
    t[0] = term[:CUT]
    t[1, : TOK - CUT] = term[CUT:]
    t[1, TOK - CUT :] = jnp.zeros((FULL - TOK, D), bf16)
    core_t = go(remote(t.at[oc], rt, as_.at[2], ar.at[2], c=oc))

    ring_pass(0, ring_s)
    ring_pass(1, ring_e)

    core_t.wait_recv()
    joint = added(t[c], rt[...]).astype(bf16)
    for g in range(8):
        tq[g] = joint[:, 128 * g : 128 * g + 128]
    tiles = []
    for g in range(1, 8):
        yo, xo = g // 4, g % 4
        ty, tx = oy if yo else y, xs[xo]
        tiles.append(go(remote(tq.at[ty * 4 + tx], tr.at[chip], ts.at[g], tr_.at[g], y=ty, x=tx)))
    tr[chip] = tq[chip]

    for copy in vector_copies + gains:
        copy.wait_recv()
    sums = svr[0] + svr[1] + svr[2] + svr[3]
    gain_sum = gpr[0]
    for m in range(1, 16):
        gain_sum = gain_sum + gpr[m]
    zero = jnp.zeros((1, SL), f32)
    for i in range(4):
        dv[i] = sums[i : i + 1]
        dv[4 + i] = svr[i, 4:5]
        dv[8 + i] = svr[i, 5:6]
    dv[12] = gain_sum[:, :SL]
    dv[13] = gain_sum[:, SL:]
    dv[14] = zero
    dv[15] = zero
    small = []
    for o, where in peers:
        e = where["z"] * 2 + where["h"]
        small.append(go(remote(dv.at[e], dvr.at[me], ds.at[o], dr.at[o], **where)))
    dvr[me] = dv[me]

    deep_s = deep_start(0, ring_s)
    deep_e = deep_start(1, ring_e)

    for copy in tiles:
        copy.wait_recv()
    tf[c] = added(*(tr[g] for g in range(8))).astype(bf16)
    finish = go(remote(tf.at[c], tf.at[c], fs, fr, c=oc))

    done = deep_sum(0, deep_s)
    shrinks = []
    for o, where in peers:
        shrinks.append(go(remote(res.at[0], sh.at[me], hs.at[o], hr.at[o], **where)))
    sh[me] = done

    for copy in small:
        copy.wait_recv()
    line = dvr[0]
    for p in range(1, 16):
        line = line + dvr[p]
    dvs[...] = line
    lines = []
    for o, where in peers:
        lines.append(go(remote(dvs, dvo.at[me], os_.at[o], or_.at[o], **where)))
    dvo[me] = line

    done = deep_sum(1, deep_e)
    goal, at = me // 4, lax.rem(me, 4)
    for o, where in peers:
        go(remote(res.at[1], ex.at[x, at], xs_.at[o], xr.at[x, at], x=goal, **where))
    mine = remote(res.at[1], ex.at[x, at], xs_.at[0], xr.at[x, at], x=goal)

    @pl.when(goal != x)
    def _():
        mine.start()

    @pl.when(goal == x)
    def _():
        ex[x, at] = done

    for copy in [finish] + shrinks + lines:
        copy.wait_recv()
    for xx in range(4):
        for p in range(4):

            @pl.when(jnp.logical_or(x != xx, me != 4 * x + p))
            def _():
                remote(res.at[1], ex.at[xx, p], xs_.at[0], xr.at[xx, p], x=goal).wait_recv()

    for copy in sent:
        copy.wait_send()

    @pl.when(goal != x)
    def _():
        mine.wait_send()


def finish_kernel(tf, sh, ex, dvo, tg, eg, sg, ing, hg, ag, og, gg):
    c = lax.axis_index("c")
    first, rest = tf[0].astype(f32), tf[1, : TOK - CUT].astype(f32)
    tg[:CUT] = jnp.where(c == 0, first[:, :64], first[:, 64:]).astype(bf16)
    tg[CUT:] = jnp.where(c == 0, rest[:, :64], rest[:, 64:]).astype(bf16)
    for i in (0, 1):
        ing[:, SL * i : SL * i + SL] = dvo[i]
        og[:, SL * i : SL * i + SL] = dvo[2 + i]
        gg[:, SL * i : SL * i + SL] = dvo[12 + i]
        for xx in range(4):
            at = 1024 * i + 256 * xx
            hg[:, at : at + 256] = dvo[4 + xx][:, 256 * i : 256 * i + 256]
            ag[:, at : at + 256] = dvo[8 + xx][:, 256 * i : 256 * i + 256]
            for p in range(4):
                eg[16 * p : 16 * p + 16, at : at + 256] = ex[xx, p, :, 256 * i : 256 * i + 256].astype(f32)
    for p in range(16):
        sg[16 * (p // 2) : 16 * (p // 2) + 16, SL * (p % 2) : SL * (p % 2) + SL] = sh[p].astype(f32)


def vmem(n):
    return [pl.BlockSpec(memory_space=pltpu.VMEM)] * n


def dma(*shape):
    return pltpu.SemaphoreType.DMA(shape)


def body(trunk, normgain, expand, shrink, inscale, hidscale, actscale, outscale, cotangent):
    S = jax.ShapeDtypeStruct
    V = pltpu.VMEM
    parts = pl.pallas_call(
        kernel,
        out_shape=[
            S((2, CUT, 128), bf16),
            S((16, 16, SL), bf16),
            S((4, 4, 16, SL), bf16),
            S((16, 1, SL), f32),
        ],
        in_specs=[pl.BlockSpec(memory_space=pl.ANY)] * 4 + vmem(5),
        out_specs=vmem(4),
        scratch_shapes=[
            V((TOK, D), bf16),
            V((4, 8, SL), f32),
            V((TOK, D), f32),
            V((TOK, D), f32),
            V((TOK, 128), f32),
            V((4, TOK, D), bf16),
            V((2, 4, 2, 64, SL), bf16),
            V((2, 2, 128, D), bf16),
            V((4, 8, SL), f32),
            V((4, TOK, D), bf16),
            V((4, TOK, SL), bf16),
            V((4, TOK, SL), f32),
            V((4, TOK, SL), f32),
            V((4, TOK, SL), f32),
            V((TOK, D), f32),
            V((SL, D), f32),
            V((D, SL), f32),
            V((2, 2, 4, 8, 16, SL), bf16),
            V((2, 4, 8, 16, SL), bf16),
            V((2, CUT, D), bf16),
            V((CUT, D), bf16),
            V((2, 4, 8, 16, SL), bf16),
            V((2, 6, 4, 16, SL), bf16),
            V((2, 2, 4, 16, SL), bf16),
            V((2, 8, 16, SL), bf16),
            V((2, 8, 16, SL), bf16),
            V((2, 16, SL), bf16),
            V((8, CUT, 128), bf16),
            V((8, CUT, 128), bf16),
            V((4, 8, SL), f32),
            V((4, 8, SL), f32),
            V((1, D), f32),
            V((16, 1, D), f32),
            V((16, 1, SL), f32),
            V((16, 1, SL), f32),
            V((1, SL), f32),
            dma(5), dma(6), dma(4, 2), dma(3, 2), dma(3, 2), dma(3), dma(3), dma(3), dma(3), dma(3), dma(3),
            dma(3), dma(3), dma(2, 6), dma(2, 6), dma(2, 8), dma(2, 8), dma(16), dma(16), dma(16), dma(4, 4),
            dma(8), dma(8), pltpu.SemaphoreType.DMA, pltpu.SemaphoreType.DMA, dma(3), dma(3), dma(16), dma(16),
            dma(16), dma(16), dma(16), dma(16),
        ],
        compiler_params=pltpu.CompilerParams(
            collective_id=0, has_side_effects=True, vmem_limit_bytes=60 * 1024 * 1024
        ),
        name="exchange_compute",
    )(
        trunk, expand, shrink, cotangent, normgain.reshape(1, D), inscale, hidscale, actscale, outscale
    )
    tg, eg, sg, ing, hg, ag, og, gg = pl.pallas_call(
        finish_kernel,
        out_shape=[
            S((TOK, 64), bf16),
            S((64, FF), f32),
            S((128, D), f32),
            S((1, D), f32),
            S((1, FF), f32),
            S((1, FF), f32),
            S((1, D), f32),
            S((1, D), f32),
        ],
        in_specs=vmem(4),
        out_specs=vmem(8),
        name="write_outputs",
    )(*parts)
    return tg, eg, sg, ing, hg, ag, og, gg.reshape(D)


def solution(mesh):
    finer = Mesh(mesh.devices.reshape(2, 4, 2, 8, 2), AXES)
    rows = P(MEMBER, None)
    in_specs = (P(DP, None), P(), rows, rows, rows, rows, rows, rows, P(MEMBER, DP, None))
    out_specs = (P(DP, MEMBER), rows, rows, rows, rows, rows, rows, P())
    return jax.shard_map(body, mesh=finer, in_specs=in_specs, out_specs=out_specs, check_vma=False)
```

time: 125 us -> 89.2 us (0.71)
  Pallas kernels: 104 us -> 86.6 us
  local copies, waits for them, and re-layouts: 16.4 us -> 1.61 us
  other arithmetic: 2.67 us -> 0 us
    pallas_call x2, Pallas kernels: 104 us -> 86.6 us  [the longest x1 84.4 us: body(): pl.pallas_call(kernel, out_shape=[S((2, CUT, 128), bf16), S((16, 16, SL),...]
    unnamed x29 -> x1, local copies, waits for them, and re-layouts: 12.4 us -> 1.61 us
    pad x2 -> x0, local copies, waits for them, and re-layouts: 3.13 us -> none  [the longest x1 2.18 us: body(): jnp.pad(trunk, pad)]
    unnamed x4 -> x0, other arithmetic: 2.67 us -> none
where the time goes in v2:
time: 89.2 us; the launch traced here: 88.8 us
  Pallas kernels  86.6 us (97%)
  local copies, waits for them, and re-layouts  1.61 us (2%)
    pallas_call x1, Pallas kernels, body(): pl.pallas_call(kernel, out_shape=[S((2, CUT, 128), bf16), S((16, 16, SL),...  84.4 us
    pallas_call x1, Pallas kernels, body(): pl.pallas_call(finish_kernel, out_shape=[S((TOK, 64), bf16), S((64, FF),...  2.15 us

profile of v2, /device:TPU:1, one launch (start us, length us, event | category | flops | bytes accessed | tf_op | source)
XLA Modules:
  0.0 88.8 jit_solution(9586753519891057154)
XLA Ops:
  0.6 84.4 %exchange_compute.1 = (bf16[2,208,128]{2,1,0:T(8,128)(2,1)}, bf16[16,16,512]{2,1,0:T(8,128)(2,1)}, bf16[4,4,16,512]{3,2,1,0:T(8,128)(2,1)}, f32[16,1,512]{2,1,0:T(1,128)}) custom-call(bf16[394,1024]{1,0:T(8,128)(2,1)} %trunk.1, bf16[64,2048]{1,0:T(8,128)(2,1)} %exp.1, bf16[128,1024]{1,0:T(8,128)(2,1)} %shr.1, bf16[1,394,1024]{2,1,0:T(8,128)(2,1)} %cot.1, ...), custom_call_target="tpu_custom_call" | custom-call | tf_op jit(solution)/shard_map/exchange_compute/pallas_call | solution.py:443
  85.1 2.1 %write_outputs.1 = (bf16[394,64]{1,0:T(8,128)(2,1)}, f32[64,2048]{1,0:T(8,128)}, f32[128,1024]{1,0:T(8,128)}, f32[1,1024]{1,0:T(1,128)}, f32[1,2048]{1,0:T(1,128...) custom-call(bf16[2,208,128]{2,1,0:T(8,128)(2,1)} %get-tuple-element.20.tf, ...), custom_call_target="tpu_custom_call" | custom-call | tf_op jit(solution)/shard_map/write_outputs/pallas_call | solution.py:502
  87.2 1.6 %copy.17 = bf16[394,64]{0,1:T(8,128)(2,1)} copy(bf16[394,64]{1,0:T(8,128)(2,1)} %get-tuple-element.32) | data formatting | bytes 100864

commit v3 on v2

--- a/solution.py
+++ b/solution.py
@@ -11,6 +11,9 @@
 DP = ("z", "h")
 TOK = 394
 CUT = 208
+EDGE = 112
+EDGE2 = 304
+PIECES = ((EDGE, CUT), (CUT, EDGE2), (0, EDGE), (EDGE2, TOK))
 FULL = 416
 D = 1024
 FF = 2048
@@ -64,7 +67,7 @@
     tbuf, vec, normed, gained, invs, cots, w1, w2, vecs, si, act, pa, actf, proj, total, sacc, eacc,
     pbuf, rbuf, t, rt, q, yb, mix, r, rz, res, tq, tr, sv, svr, gp, gpr, dv, dvr, dvs,
     ls, cs, cr, ws, wr, vs, vr, ss, sr, es, er,
-    as_, ar, ys, yr, zs, zr, hs, hr, xs_, xr, ts, tr_, fs, fr, bs, br, gs, gr, ds, dr, os_, or_,
+    as_, ar, ys, yr, zs, zr, hs, hr, xs_, xr, ts, tr_, fs, fr, bs, br, gs, gr, ds, dr, os_, or_, heard,
 ):
     y, x, c, z, h = (lax.axis_index(a) for a in AXES)
     xs = [lax.rem(x + o, 4) for o in range(4)]
@@ -81,15 +84,23 @@
 
     barrier = pltpu.get_barrier_semaphore()
 
-    @pl.loop(1, 64)
-    def _(o):
-        e = lax.rem(me + lax.rem(o, 16), 16)
-        greet(barrier, x=lax.rem(x + o // 16, 4), z=e // 2, h=lax.rem(e, 2))
-
-    for yo, co in ((0, 1), (1, 0), (1, 1)):
-        for xo in range(4):
-            greet(barrier, y=oy if yo else y, x=xs[xo], c=oc if co else c)
+    for yo in (0, 1):
+        for co in (0, 1):
+            for xo in range(4):
+                if yo or co or xo:
+                    greet(barrier, y=oy if yo else y, x=xs[xo], c=oc if co else c)
     greet(barrier, y=oy, h=1 - h)
+    greet(barrier, h=1 - h)
+    above, below = lax.rem(z + 1, 8), lax.rem(z + 7, 8)
+    greet(barrier, z=above)
+    greet(barrier, z=below)
+
+    def tell_z(i):
+        greet(heard.at[i], z=above)
+        greet(heard.at[i], z=below)
+
+    def told(i, n):
+        pl.semaphore_wait(heard.at[i], n)
 
     here = [
         pltpu.make_async_copy(trunk, tbuf, ls.at[0]),
@@ -114,7 +125,8 @@
             vec[xx, 4:5, 256 * i : 256 * i + 256] = hidscale[:, at : at + 256]
             vec[xx, 5:6, 256 * i : 256 * i + 256] = actscale[:, at : at + 256]
         vec[xx, 6:8] = jnp.zeros((2, SL), f32)
-    pl.semaphore_wait(barrier, 76)
+    pl.semaphore_wait(barrier, 19)
+    tell_z(0)
 
     slot_of = {1: 1, 3: 2, 2: 3}
     vec_copies, exp_copies = {}, {}
@@ -166,13 +178,18 @@
         si[k] = (gained[...] * row(vecs[k], 0)).astype(bf16)
 
     right_a.wait_recv()
-    fwd_a = go(remote(cots.at[1, a], cots.at[3, a], cs.at[4], cr.at[3, 0], x=xs[1]))
     left_b.wait_recv()
-    fwd_b = go(remote(cots.at[2, b], cots.at[3, b], cs.at[5], cr.at[3, 1], x=xs[3]))
+    fwd = []
+    for i, (lo, hi) in enumerate(PIECES):
+        src, to = ((1, xs[1]), (2, xs[3]))[i % 2]
+        piece = pl.ds(lo, hi - lo)
+        fwd.append(go(remote(cots.at[src, piece], cots.at[3, piece], cs.at[4 + i], cr.at[3, i], x=to)))
     exp_y.wait_recv()
     exp_f = go(remote(w1.at[oy, :, c], w1.at[oy, :, c], es.at[2], er.at[2], c=oc))
     for copy in (shr_c, exp_c, shr_f, exp_f):
         copy.wait_recv()
+    told(0, 2)
+    tell_z(1)
 
     @pl.loop(0, 4)
     def _(k):
@@ -184,32 +201,47 @@
         act[k] = (active * v[5:6]).astype(bf16)
         pa[k] = slope * v[5:6]
 
-    def back_part(k):
+    told(1, 2)
+    tell_z(2)
+
+    def take(ref, k, rows):
+        blocks = [ref[k, lo:hi] for lo, hi in rows]
+        return blocks[0] if len(blocks) == 1 else jnp.concatenate(blocks, axis=0)
+
+    def back_part(k, rows, first):
         v = vecs[k]
         scale_out = row(v, 2)
         second = w2[...].reshape(SL, D)
-        seed = cots[k]
+        seed = take(cots, k, rows)
         scaled_cot = (seed.astype(f32) * scale_out).astype(bf16)
         back = dot(scaled_cot, second, 1, 1)
-        grad_act = jnp.sum(back * actf[k], axis=0, keepdims=True)
-        back_hidden = back * pa[k]
-        grad_hid = jnp.sum(back_hidden * proj[k], axis=0, keepdims=True)
+        grad_act = jnp.sum(back * take(actf, k, rows), axis=0, keepdims=True)
+        back_hidden = back * take(pa, k, rows)
+        grad_hid = jnp.sum(back_hidden * take(proj, k, rows), axis=0, keepdims=True)
         back_proj = (back_hidden * v[4:5]).astype(bf16)
-        both = dot(act[k], seed, 0, 0)
+        both = dot(take(act, k, rows), seed, 0, 0)
         sacc[...] += both * scale_out
         grad_out = jnp.sum(second.astype(f32) * both, axis=0, keepdims=True)
         zero = jnp.zeros((2, SL), f32)
-        sv[k, 2:8] = jnp.concatenate([grad_out[:, :SL], grad_out[:, SL:], grad_hid, grad_act, zero], axis=0)
+        lines = jnp.concatenate([grad_out[:, :SL], grad_out[:, SL:], grad_hid, grad_act, zero], axis=0)
+        sv[k, 2:8] = lines if first else sv[k, 2:8] + lines
         return back_proj
 
-    def expand_part(k, back_proj):
-        eacc[...] += dot(si[k], back_proj, 0, 0)
-
-    def norm_part(k, back_proj):
+    def expand_part(k, rows, back_proj):
+        eacc[...] += dot(take(si, k, rows), back_proj, 0, 0)
+
+    def norm_part(k, rows, first, back_proj):
         back_norm = dot(back_proj, w1[...].reshape(D, SL), 1, 1)
-        grad_in = jnp.sum(back_norm * gained[...], axis=0, keepdims=True)
-        total[...] += back_norm * row(vecs[k], 0)
-        sv[k, 0:2] = jnp.concatenate([grad_in[:, :SL], grad_in[:, SL:]], axis=0)
+        share = back_norm * row(vecs[k], 0)
+        grad_in = 0.0
+        at = 0
+        for lo, hi in rows:
+            end = at + hi - lo
+            grad_in = grad_in + jnp.sum(back_norm[at:end] * gained[lo:hi], axis=0, keepdims=True)
+            total[lo:hi] += share[at:end]
+            at = end
+        lines = jnp.concatenate([grad_in[:, :SL], grad_in[:, SL:]], axis=0)
+        sv[k, 0:2] = lines if first else sv[k, 0:2] + lines
 
     @pl.loop(0, 3)
     def _(k):
@@ -221,9 +253,10 @@
         def _():
             left_a.wait_recv()
 
-        back_proj = back_part(k)
-        expand_part(k, back_proj)
-        norm_part(k, back_proj)
+        every = ((0, TOK),)
+        back_proj = back_part(k, every, True)
+        expand_part(k, every, back_proj)
+        norm_part(k, every, True, back_proj)
 
     right, left, far = (lax.rem(place + o, 4) for o in (1, 3, 2))
     to_right = dict(y=lax.rem(right, 2), h=right // 2)
@@ -275,9 +308,20 @@
         e = lax.rem(me + o, 16)
         peers.append((o, dict(z=e // 2, h=lax.rem(e, 2))))
 
-    fwd_a.wait_recv()
-    fwd_b.wait_recv()
-    back_proj = back_part(3)
+    told(2, 2)
+    greet(heard.at[3], h=1 - h)
+    fwd[0].wait_recv()
+    fwd[1].wait_recv()
+    mid, ends = ((EDGE, EDGE2),), ((0, EDGE), (EDGE2, TOK))
+    back_proj = back_part(3, mid, True)
+    expand_part(3, mid, back_proj)
+    norm_part(3, mid, True, back_proj)
+    told(3, 1)
+    for o in (1, 2, 3):
+        greet(heard.at[4], x=xs[o])
+    fwd[2].wait_recv()
+    fwd[3].wait_recv()
+    back_proj = back_part(3, ends, False)
     for cc in (0, 1):
         for hh in (0, 1):
             for yy in (0, 1):
@@ -285,7 +329,7 @@
                 block = sacc[at : at + 128, SL * hh : SL * hh + SL]
                 pbuf[0, cc, 2 * hh + yy] = block.astype(bf16).reshape(8, 16, SL)
     core_s = core_step(0)
-    expand_part(3, back_proj)
+    expand_part(3, ends, back_proj)
     for cc in (0, 1):
         for hh in (0, 1):
             for yy in (0, 1):
@@ -294,7 +338,7 @@
                     pbuf[1, cc, 2 * hh + yy, zz] = eacc[at : at + 16].astype(bf16)
     core_e = core_step(1)
     ring_s = ring_start(0, core_s)
-    norm_part(3, back_proj)
+    norm_part(3, ends, False, back_proj)
     ring_e = ring_start(1, core_e)
 
     vector_copies = []
@@ -354,6 +398,7 @@
         small.append(go(remote(dv.at[e], dvr.at[me], ds.at[o], dr.at[o], **where)))
     dvr[me] = dv[me]
 
+    told(4, 3)
     deep_s = deep_start(0, ring_s)
     deep_e = deep_start(1, ring_e)
 
@@ -412,9 +457,8 @@
 
 def finish_kernel(tf, sh, ex, dvo, tg, eg, sg, ing, hg, ag, og, gg):
     c = lax.axis_index("c")
-    first, rest = tf[0].astype(f32), tf[1, : TOK - CUT].astype(f32)
-    tg[:CUT] = jnp.where(c == 0, first[:, :64], first[:, 64:]).astype(bf16)
-    tg[CUT:] = jnp.where(c == 0, rest[:, :64], rest[:, 64:]).astype(bf16)
+    turned = tf[...].reshape(FULL, 128).astype(f32).T
+    tg[...] = jnp.where(c == 0, turned[:64], turned[64:])[:, :TOK].astype(bf16)
     for i in (0, 1):
         ing[:, SL * i : SL * i + SL] = dvo[i]
         og[:, SL * i : SL * i + SL] = dvo[2 + i]
@@ -487,10 +531,10 @@
             V((16, 1, SL), f32),
             V((16, 1, SL), f32),
             V((1, SL), f32),
-            dma(5), dma(6), dma(4, 2), dma(3, 2), dma(3, 2), dma(3), dma(3), dma(3), dma(3), dma(3), dma(3),
+            dma(5), dma(8), dma(4, 4), dma(3, 2), dma(3, 2), dma(3), dma(3), dma(3), dma(3), dma(3), dma(3),
             dma(3), dma(3), dma(2, 6), dma(2, 6), dma(2, 8), dma(2, 8), dma(16), dma(16), dma(16), dma(4, 4),
             dma(8), dma(8), pltpu.SemaphoreType.DMA, pltpu.SemaphoreType.DMA, dma(3), dma(3), dma(16), dma(16),
-            dma(16), dma(16), dma(16), dma(16),
+            dma(16), dma(16), dma(16), dma(16), pltpu.SemaphoreType.REGULAR((5,)),
         ],
         compiler_params=pltpu.CompilerParams(
             collective_id=0, has_side_effects=True, vmem_limit_bytes=60 * 1024 * 1024
@@ -502,7 +546,7 @@
     tg, eg, sg, ing, hg, ag, og, gg = pl.pallas_call(
         finish_kernel,
         out_shape=[
-            S((TOK, 64), bf16),
+            S((64, TOK), bf16),
             S((64, FF), f32),
             S((128, D), f32),
             S((1, D), f32),
@@ -515,7 +559,7 @@
         out_specs=vmem(8),
         name="write_outputs",
     )(*parts)
-    return tg, eg, sg, ing, hg, ag, og, gg.reshape(D)
+    return tg.T, eg, sg, ing, hg, ag, og, gg.reshape(D)
 
 
 def solution(mesh):

time: 89.2 us -> 84.2 us (0.944)
  Pallas kernels: 86.6 us -> 82.6 us
  local copies, waits for them, and re-layouts: 1.61 us -> 0 us
    pallas_call x1, Pallas kernels: 84.4 us -> 80.4 us  [body(): pl.pallas_call(kernel, out_shape=[S((2, CUT, 128), bf16), S((16, 16, SL),...]
    unnamed x1 -> x0, local copies, waits for them, and re-layouts: 1.61 us -> none
where the time goes in v3:
time: 84.2 us; the launch traced here: 83.2 us
  Pallas kernels  82.6 us (98%)
    pallas_call x1, Pallas kernels, body(): pl.pallas_call(kernel, out_shape=[S((2, CUT, 128), bf16), S((16, 16, SL),...  80.4 us
    pallas_call x1, Pallas kernels, body(): pl.pallas_call(finish_kernel, out_shape=[S((64, TOK), bf16), S((64, FF),...  2.18 us

profile of v3, /device:TPU:1, one launch (start us, length us, event | category | flops | bytes accessed | tf_op | source)
XLA Modules:
  0.0 83.2 jit_solution(11927969251481951429)
XLA Ops:
  0.6 80.4 %exchange_compute.1 = (bf16[2,208,128]{2,1,0:T(8,128)(2,1)}, bf16[16,16,512]{2,1,0:T(8,128)(2,1)}, bf16[4,4,16,512]{3,2,1,0:T(8,128)(2,1)}, f32[16,1,512]{2,1,0:T(1,128)}) custom-call(bf16[394,1024]{1,0:T(8,128)(2,1)} %trunk.1, bf16[64,2048]{1,0:T(8,128)(2,1)} %exp.1, bf16[128,1024]{1,0:T(8,128)(2,1)} %shr.1, bf16[1,394,1024]{2,1,0:T(8,128)(2,1)} %cot.1, ...), custom_call_target="tpu_custom_call" | custom-call | tf_op jit(solution)/shard_map/exchange_compute/pallas_call | solution.py:487
  81.0 2.2 %write_outputs.1 = (bf16[64,394]{1,0:T(8,128)(2,1)}, f32[64,2048]{1,0:T(8,128)}, f32[128,1024]{1,0:T(8,128)}, f32[1,1024]{1,0:T(1,128)}, f32[1,2048]{1,0:T(1,128...) custom-call(bf16[2,208,128]{2,1,0:T(8,128)(2,1)} %get-tuple-element.20.tf, ...), custom_call_target="tpu_custom_call" | custom-call | tf_op jit(solution)/shard_map/write_outputs/pallas_call | solution.py:546

commit v4 on v3

--- a/solution.py
+++ b/solution.py
@@ -11,9 +11,10 @@
 DP = ("z", "h")
 TOK = 394
 CUT = 208
-EDGE = 112
-EDGE2 = 304
-PIECES = ((EDGE, CUT), (CUT, EDGE2), (0, EDGE), (EDGE2, TOK))
+EDGE = 96
+SEAM = 176
+EDGE2 = 288
+PIECES = ((EDGE, SEAM), (SEAM, EDGE2), (0, EDGE), (EDGE2, TOK))
 FULL = 416
 D = 1024
 FF = 2048
@@ -67,7 +68,7 @@
     tbuf, vec, normed, gained, invs, cots, w1, w2, vecs, si, act, pa, actf, proj, total, sacc, eacc,
     pbuf, rbuf, t, rt, q, yb, mix, r, rz, res, tq, tr, sv, svr, gp, gpr, dv, dvr, dvs,
     ls, cs, cr, ws, wr, vs, vr, ss, sr, es, er,
-    as_, ar, ys, yr, zs, zr, hs, hr, xs_, xr, ts, tr_, fs, fr, bs, br, gs, gr, ds, dr, os_, or_, heard,
+    as_, ar, ys, yr, zs, zr, hs, hr, ts, tr_, fs, fr, bs, br, gs, gr, ds, dr, os_, or_, heard,
 ):
     y, x, c, z, h = (lax.axis_index(a) for a in AXES)
     xs = [lax.rem(x + o, 4) for o in range(4)]
@@ -142,7 +143,7 @@
         ))
     shr_y = go(remote(shr, w2.at[y, c], ss.at[0], sr.at[0], y=oy))
     shr_c = go(remote(shr, w2.at[y, c], ss.at[1], sr.at[1], c=oc))
-    a, b = pl.ds(0, CUT), pl.ds(CUT, TOK - CUT)
+    a, b = pl.ds(0, SEAM), pl.ds(SEAM, TOK - SEAM)
     right_a = go(remote(cot.at[0, a], cots.at[1, a], cs.at[0], cr.at[1, 0], x=xs[1]))
     left_b = go(remote(cot.at[0, b], cots.at[2, b], cs.at[2], cr.at[2, 1], x=xs[3]))
     right_b = go(remote(cot.at[0, b], cots.at[1, b], cs.at[1], cr.at[1, 1], x=xs[1]))
@@ -290,10 +291,23 @@
         r[i, 0:4] = added(q[i, place, 0:4], yb[i, 3], yb[i, 4]).astype(bf16)
         r[i, 4:8] = added(q[i, place, 4:8], yb[i, 2], yb[i, 5]).astype(bf16)
         out = []
-        for o in (4, 3, 5, 2, 6, 1, 7):
+        if i == 0:
+            for o in (4, 3, 5, 2, 6, 1, 7):
+                e = lax.rem(z + o, 8)
+                out.append(go(remote(r.at[0, e], rz.at[0, z], zs.at[0, o], zr.at[0, o], z=e)))
+            rz[0, z] = r[0, z]
+            return out
+        mine = pl.ds(pl.multiple_of(128 * x, 128), 128)
+        for o in (4, 3, 5, 2, 6, 1, 7, 0):
             e = lax.rem(z + o, 8)
-            out.append(go(remote(r.at[i, e], rz.at[i, z], zs.at[i, o], zr.at[i, o], z=e)))
-        rz[i, z] = r[i, z]
+            for xo in range(4):
+                if o or xo:
+                    block = pl.ds(pl.multiple_of(128 * xs[xo], 128), 128)
+                    out.append(go(remote(
+                        r.at[1, e, :, block], rz.at[1, z, :, mine], zs.at[1 + xo, o], zr.at[1 + xo, o],
+                        z=e, x=xs[xo],
+                    )))
+        rz[1, z, :, mine] = r[1, z, :, mine]
         return out
 
     def deep_sum(i, copies):
@@ -333,9 +347,13 @@
     for cc in (0, 1):
         for hh in (0, 1):
             for yy in (0, 1):
-                for zz in range(8):
-                    at = ((yy * 4 + zz // 2) * 2 + cc) * 64 + zz % 2 * 32 + hh * 16
-                    pbuf[1, cc, 2 * hh + yy, zz] = eacc[at : at + 16].astype(bf16)
+                for xx in range(4):
+                    at = ((yy * 4 + xx) * 2 + cc) * 64
+                    for zz in range(8):
+                        top_row, lane = at + zz // 2 * 16, (zz % 2 * 2 + hh) * 128
+                        pbuf[1, cc, 2 * hh + yy, zz, :, 128 * xx : 128 * xx + 128] = eacc[
+                            top_row : top_row + 16, lane : lane + 128
+                        ].astype(bf16)
     core_e = core_step(1)
     ring_s = ring_start(0, core_s)
     norm_part(3, ends, False, back_proj)
@@ -377,6 +395,9 @@
         tiles.append(go(remote(tq.at[ty * 4 + tx], tr.at[chip], ts.at[g], tr_.at[g], y=ty, x=tx)))
     tr[chip] = tq[chip]
 
+    told(4, 3)
+    deep_s = deep_start(0, ring_s)
+
     for copy in vector_copies + gains:
         copy.wait_recv()
     sums = svr[0] + svr[1] + svr[2] + svr[3]
@@ -398,20 +419,12 @@
         small.append(go(remote(dv.at[e], dvr.at[me], ds.at[o], dr.at[o], **where)))
     dvr[me] = dv[me]
 
-    told(4, 3)
-    deep_s = deep_start(0, ring_s)
     deep_e = deep_start(1, ring_e)
 
     for copy in tiles:
         copy.wait_recv()
     tf[c] = added(*(tr[g] for g in range(8))).astype(bf16)
     finish = go(remote(tf.at[c], tf.at[c], fs, fr, c=oc))
-
-    done = deep_sum(0, deep_s)
-    shrinks = []
-    for o, where in peers:
-        shrinks.append(go(remote(res.at[0], sh.at[me], hs.at[o], hr.at[o], **where)))
-    sh[me] = done
 
     for copy in small:
         copy.wait_recv()
@@ -424,35 +437,49 @@
         lines.append(go(remote(dvs, dvo.at[me], os_.at[o], or_.at[o], **where)))
     dvo[me] = line
 
+    outs = (sh, ex)
+
+    def spread(i):
+        copies = {}
+        for o in (2, 6, 1, 7, 0):
+            e = lax.rem(z + o, 8)
+            for ho in (0, 1):
+                if o or ho:
+                    copies[o, ho] = go(remote(
+                        res.at[i], outs[i].at[me], hs.at[i, o, ho], hr.at[i, o, ho],
+                        z=e, h=1 - h if ho else h,
+                    ))
+        return copies
+
+    def relay(i, copies):
+        for o, further in ((2, (4, 3)), (6, (5,))):
+            for ho in (0, 1):
+                copies[o, ho].wait_recv()
+                place = lax.rem(z + 8 - o, 8) * 2 + (1 - h if ho else h)
+                for far_o in further:
+                    copies[far_o, ho] = go(remote(
+                        outs[i].at[place], outs[i].at[place], hs.at[i, far_o, ho], hr.at[i, far_o, ho],
+                        z=lax.rem(z + far_o - o + 8, 8),
+                    ))
+
+    done = deep_sum(0, deep_s)
+    spread_s = spread(0)
+    sh[me] = done
     done = deep_sum(1, deep_e)
-    goal, at = me // 4, lax.rem(me, 4)
-    for o, where in peers:
-        go(remote(res.at[1], ex.at[x, at], xs_.at[o], xr.at[x, at], x=goal, **where))
-    mine = remote(res.at[1], ex.at[x, at], xs_.at[0], xr.at[x, at], x=goal)
-
-    @pl.when(goal != x)
-    def _():
-        mine.start()
-
-    @pl.when(goal == x)
-    def _():
-        ex[x, at] = done
-
-    for copy in [finish] + shrinks + lines:
+    spread_e = spread(1)
+    ex[me] = done
+    relay(0, spread_s)
+    relay(1, spread_e)
+
+    for copy in [finish] + lines:
         copy.wait_recv()
-    for xx in range(4):
-        for p in range(4):
-
-            @pl.when(jnp.logical_or(x != xx, me != 4 * x + p))
-            def _():
-                remote(res.at[1], ex.at[xx, p], xs_.at[0], xr.at[xx, p], x=goal).wait_recv()
+    for copies in (spread_s, spread_e):
+        for (o, ho), copy in copies.items():
+            if o not in (2, 6):
+                copy.wait_recv()
 
     for copy in sent:
         copy.wait_send()
-
-    @pl.when(goal != x)
-    def _():
-        mine.wait_send()
 
 
 def finish_kernel(tf, sh, ex, dvo, tg, eg, sg, ing, hg, ag, og, gg):
@@ -467,9 +494,11 @@
             at = 1024 * i + 256 * xx
             hg[:, at : at + 256] = dvo[4 + xx][:, 256 * i : 256 * i + 256]
             ag[:, at : at + 256] = dvo[8 + xx][:, 256 * i : 256 * i + 256]
-            for p in range(4):
-                eg[16 * p : 16 * p + 16, at : at + 256] = ex[xx, p, :, 256 * i : 256 * i + 256].astype(f32)
     for p in range(16):
+        low, lane = p // 4 * 16, p % 4 // 2 * 1024 + p % 2 * 128
+        for xx in range(4):
+            at = lane + 256 * xx
+            eg[low : low + 16, at : at + 128] = ex[p, :, 128 * xx : 128 * xx + 128].astype(f32)
         sg[16 * (p // 2) : 16 * (p // 2) + 16, SL * (p % 2) : SL * (p % 2) + SL] = sh[p].astype(f32)
 
 
@@ -489,7 +518,7 @@
         out_shape=[
             S((2, CUT, 128), bf16),
             S((16, 16, SL), bf16),
-            S((4, 4, 16, SL), bf16),
+            S((16, 16, SL), bf16),
             S((16, 1, SL), f32),
         ],
         in_specs=[pl.BlockSpec(memory_space=pl.ANY)] * 4 + vmem(5),
@@ -532,7 +561,7 @@
             V((16, 1, SL), f32),
             V((1, SL), f32),
             dma(5), dma(8), dma(4, 4), dma(3, 2), dma(3, 2), dma(3), dma(3), dma(3), dma(3), dma(3), dma(3),
-            dma(3), dma(3), dma(2, 6), dma(2, 6), dma(2, 8), dma(2, 8), dma(16), dma(16), dma(16), dma(4, 4),
+            dma(3), dma(3), dma(2, 6), dma(2, 6), dma(5, 8), dma(5, 8), dma(2, 8, 2), dma(2, 8, 2),
             dma(8), dma(8), pltpu.SemaphoreType.DMA, pltpu.SemaphoreType.DMA, dma(3), dma(3), dma(16), dma(16),
             dma(16), dma(16), dma(16), dma(16), pltpu.SemaphoreType.REGULAR((5,)),
         ],

time: 84.2 us -> 82.5 us (0.980)
  Pallas kernels: 82.6 us -> 81.1 us
    pallas_call x1, Pallas kernels: 80.4 us -> 79 us  [body(): pl.pallas_call(kernel, out_shape=[S((2, CUT, 128), bf16), S((16, 16, SL),...]
where the time goes in v4:
time: 82.5 us; the launch traced here: 81.8 us
  Pallas kernels  81.1 us (98%)
    pallas_call x1, Pallas kernels, body(): pl.pallas_call(kernel, out_shape=[S((2, CUT, 128), bf16), S((16, 16, SL),...  79 us
    pallas_call x1, Pallas kernels, body(): pl.pallas_call(finish_kernel, out_shape=[S((64, TOK), bf16), S((64, FF),...  2.17 us

profile of v4, /device:TPU:1, one launch (start us, length us, event | category | flops | bytes accessed | tf_op | source)
XLA Modules:
  0.0 81.8 jit_solution(1844491708661866714)
XLA Ops:
  0.6 79.0 %exchange_compute.1 = (bf16[2,208,128]{2,1,0:T(8,128)(2,1)}, bf16[16,16,512]{2,1,0:T(8,128)(2,1)}, bf16[16,16,512]{2,1,0:T(8,128)(2,1)}, f32[16,1,512]{2,1,0:T(1,128)}) custom-call(bf16[394,1024]{1,0:T(8,128)(2,1)} %trunk.1, bf16[64,2048]{1,0:T(8,128)(2,1)} %exp.1, bf16[128,1024]{1,0:T(8,128)(2,1)} %shr.1, bf16[1,394,1024]{2,1,0:T(8,128)(2,1)} %cot.1, ...), custom_call_target="tpu_custom_call" | custom-call | tf_op jit(solution)/shard_map/exchange_compute/pallas_call | solution.py:516
  79.6 2.2 %write_outputs.1 = (bf16[64,394]{1,0:T(8,128)(2,1)}, f32[64,2048]{1,0:T(8,128)}, f32[128,1024]{1,0:T(8,128)}, f32[1,1024]{1,0:T(1,128)}, f32[1,2048]{1,0:T(1,128...) custom-call(bf16[2,208,128]{2,1,0:T(8,128)(2,1)} %get-tuple-element.20.tf, ...), custom_call_target="tpu_custom_call" | custom-call | tf_op jit(solution)/shard_map/write_outputs/pallas_call | solution.py:575

commit v5 on v4

--- a/solution.py
+++ b/solution.py
@@ -12,7 +12,7 @@
 TOK = 394
 CUT = 208
 EDGE = 96
-SEAM = 176
+SEAM = 192
 EDGE2 = 288
 PIECES = ((EDGE, SEAM), (SEAM, EDGE2), (0, EDGE), (EDGE2, TOK))
 FULL = 416
@@ -63,9 +63,9 @@
 
 
 def kernel(
-    trunk, exp, shr, cot, gain, inscale, hidscale, actscale, outscale,
+    trunk, exp, shr, cot, gain_in, in_in, hid_in, act_in, out_in,
     tf, sh, ex, dvo,
-    tbuf, vec, normed, gained, invs, cots, w1, w2, vecs, si, act, pa, actf, proj, total, sacc, eacc,
+    gain, inscale, hidscale, actscale, outscale, tbuf, vec, normed, gained, invs, cots, w1, w2, vecs, si, act, pa, actf, proj, total, sacc, eacc,
     pbuf, rbuf, t, rt, q, yb, mix, r, rz, res, tq, tr, sv, svr, gp, gpr, dv, dvr, dvs,
     ls, cs, cr, ws, wr, vs, vr, ss, sr, es, er,
     as_, ar, ys, yr, zs, zr, hs, hr, ts, tr_, fs, fr, bs, br, gs, gr, ds, dr, os_, or_, heard,
@@ -116,16 +116,13 @@
                 ls.at[3 + half],
             )
         )
-    for copy in here:
+    lines = []
+    for i, (src, dst) in enumerate(
+        ((in_in, inscale), (hid_in, hidscale), (act_in, actscale), (out_in, outscale), (gain_in, gain))
+    ):
+        lines.append(pltpu.make_async_copy(src, dst, ls.at[5 + i]))
+    for copy in lines + here:
         copy.start()
-    for xx in range(4):
-        for i in (0, 1):
-            vec[xx, i : i + 1] = inscale[:, SL * i : SL * i + SL]
-            vec[xx, 2 + i : 3 + i] = outscale[:, SL * i : SL * i + SL]
-            at = 1024 * i + 256 * xx
-            vec[xx, 4:5, 256 * i : 256 * i + 256] = hidscale[:, at : at + 256]
-            vec[xx, 5:6, 256 * i : 256 * i + 256] = actscale[:, at : at + 256]
-        vec[xx, 6:8] = jnp.zeros((2, SL), f32)
     pl.semaphore_wait(barrier, 19)
     tell_z(0)
 
@@ -138,11 +135,22 @@
                 w1.at[y, x, c, :, pl.ds(256 * half, 256)],
                 ws.at[o - 1, half], wr.at[o - 1, half], x=xs[o],
             ))
+    shr_y = go(remote(shr, w2.at[y, c], ss.at[0], sr.at[0], y=oy))
+    shr_c = go(remote(shr, w2.at[y, c], ss.at[1], sr.at[1], c=oc))
+    for copy in lines:
+        copy.wait()
+    for xx in range(4):
+        for i in (0, 1):
+            vec[xx, i : i + 1] = inscale[:, SL * i : SL * i + SL]
+            vec[xx, 2 + i : 3 + i] = outscale[:, SL * i : SL * i + SL]
+            at = 1024 * i + 256 * xx
+            vec[xx, 4:5, 256 * i : 256 * i + 256] = hidscale[:, at : at + 256]
+            vec[xx, 5:6, 256 * i : 256 * i + 256] = actscale[:, at : at + 256]
+        vec[xx, 6:8] = jnp.zeros((2, SL), f32)
+    for o in (1, 3, 2):
         vec_copies[o] = go(remote(
             vec.at[xs[o]], vecs.at[slot_of[o]], vs.at[o - 1], vr.at[o - 1], x=xs[o]
         ))
-    shr_y = go(remote(shr, w2.at[y, c], ss.at[0], sr.at[0], y=oy))
-    shr_c = go(remote(shr, w2.at[y, c], ss.at[1], sr.at[1], c=oc))
     a, b = pl.ds(0, SEAM), pl.ds(SEAM, TOK - SEAM)
     right_a = go(remote(cot.at[0, a], cots.at[1, a], cs.at[0], cr.at[1, 0], x=xs[1]))
     left_b = go(remote(cot.at[0, b], cots.at[2, b], cs.at[2], cr.at[2, 1], x=xs[3]))
@@ -383,6 +391,9 @@
 
     ring_pass(0, ring_s)
     ring_pass(1, ring_e)
+    told(4, 3)
+    deep_s = deep_start(0, ring_s)
+    deep_e = deep_start(1, ring_e)
 
     core_t.wait_recv()
     joint = added(t[c], rt[...]).astype(bf16)
@@ -394,9 +405,6 @@
         ty, tx = oy if yo else y, xs[xo]
         tiles.append(go(remote(tq.at[ty * 4 + tx], tr.at[chip], ts.at[g], tr_.at[g], y=ty, x=tx)))
     tr[chip] = tq[chip]
-
-    told(4, 3)
-    deep_s = deep_start(0, ring_s)
 
     for copy in vector_copies + gains:
         copy.wait_recv()
@@ -419,24 +427,6 @@
         small.append(go(remote(dv.at[e], dvr.at[me], ds.at[o], dr.at[o], **where)))
     dvr[me] = dv[me]
 
-    deep_e = deep_start(1, ring_e)
-
-    for copy in tiles:
-        copy.wait_recv()
-    tf[c] = added(*(tr[g] for g in range(8))).astype(bf16)
-    finish = go(remote(tf.at[c], tf.at[c], fs, fr, c=oc))
-
-    for copy in small:
-        copy.wait_recv()
-    line = dvr[0]
-    for p in range(1, 16):
-        line = line + dvr[p]
-    dvs[...] = line
-    lines = []
-    for o, where in peers:
-        lines.append(go(remote(dvs, dvo.at[me], os_.at[o], or_.at[o], **where)))
-    dvo[me] = line
-
     outs = (sh, ex)
 
     def spread(i):
@@ -468,6 +458,23 @@
     done = deep_sum(1, deep_e)
     spread_e = spread(1)
     ex[me] = done
+
+    for copy in tiles:
+        copy.wait_recv()
+    tf[c] = added(*(tr[g] for g in range(8))).astype(bf16)
+    finish = go(remote(tf.at[c], tf.at[c], fs, fr, c=oc))
+
+    for copy in small:
+        copy.wait_recv()
+    line = dvr[0]
+    for p in range(1, 16):
+        line = line + dvr[p]
+    dvs[...] = line
+    lines = []
+    for o, where in peers:
+        lines.append(go(remote(dvs, dvo.at[me], os_.at[o], or_.at[o], **where)))
+    dvo[me] = line
+
     relay(0, spread_s)
     relay(1, spread_e)
 
@@ -516,14 +523,19 @@
     parts = pl.pallas_call(
         kernel,
         out_shape=[
-            S((2, CUT, 128), bf16),
-            S((16, 16, SL), bf16),
-            S((16, 16, SL), bf16),
-            S((16, 1, SL), f32),
+            V((2, CUT, 128), bf16),
+            V((16, 16, SL), bf16),
+            V((16, 16, SL), bf16),
+            V((16, 1, SL), f32),
         ],
-        in_specs=[pl.BlockSpec(memory_space=pl.ANY)] * 4 + vmem(5),
+        in_specs=[pl.BlockSpec(memory_space=pl.ANY)] * 9,
         out_specs=vmem(4),
         scratch_shapes=[
+            V((1, D), f32),
+            V((1, D), f32),
+            V((1, FF), f32),
+            V((1, FF), f32),
+            V((1, D), f32),
             V((TOK, D), bf16),
             V((4, 8, SL), f32),
             V((TOK, D), f32),
@@ -560,7 +572,7 @@
             V((16, 1, SL), f32),
             V((16, 1, SL), f32),
             V((1, SL), f32),
-            dma(5), dma(8), dma(4, 4), dma(3, 2), dma(3, 2), dma(3), dma(3), dma(3), dma(3), dma(3), dma(3),
+            dma(10), dma(8), dma(4, 4), dma(3, 2), dma(3, 2), dma(3), dma(3), dma(3), dma(3), dma(3), dma(3),
             dma(3), dma(3), dma(2, 6), dma(2, 6), dma(5, 8), dma(5, 8), dma(2, 8, 2), dma(2, 8, 2),
             dma(8), dma(8), pltpu.SemaphoreType.DMA, pltpu.SemaphoreType.DMA, dma(3), dma(3), dma(16), dma(16),
             dma(16), dma(16), dma(16), dma(16), pltpu.SemaphoreType.REGULAR((5,)),

time: 82.5 us -> 82.7 us (level)
  local copies, waits for them, and re-layouts: 0 us -> 2.63 us
  Pallas kernels: 81.1 us -> 79.3 us
    unnamed x0 -> x8, local copies, waits for them, and re-layouts: none -> 2.63 us
    pallas_call x1, Pallas kernels: 79 us -> 77.1 us  [body(): pl.pallas_call(kernel, out_shape=[V((2, CUT, 128), bf16), V((16, 16, SL),...]
where the time goes in v5:
time: 82.7 us; the launch traced here: 82.6 us
  Pallas kernels  79.3 us (96%)
  local copies, waits for them, and re-layouts  2.63 us (3%)
    pallas_call x1, Pallas kernels, body(): pl.pallas_call(kernel, out_shape=[V((2, CUT, 128), bf16), V((16, 16, SL),...  77.1 us
    unnamed x8, local copies, waits for them, and re-layouts  2.63 us
    pallas_call x1, Pallas kernels, body(): pl.pallas_call(finish_kernel, out_shape=[S((64, TOK), bf16), S((64, FF),...  2.17 us

profile of v5, /device:TPU:1, one launch (start us, length us, event | category | flops | bytes accessed | tf_op | source)
XLA Modules:
  0.0 82.6 jit_solution(16834078155184356082)
XLA Ops:
  0.6 77.1 %exchange_compute.1 = (bf16[2,208,128]{2,1,0:T(8,128)(2,1)S(1)}, bf16[16,16,512]{2,1,0:T(8,128)(2,1)S(1)}, bf16[16,16,512]{2,1,0:T(8,128)(2,1)S(1)}, f32[16,1,512]{2,1,0:T(1,128)S(1)}) custom-call(bf16[394,1024]{1,0:T(8,128)(2,1)} %trunk.1, bf16[64,2048]{1,0:T(8,128)(2,1)} %exp.1, bf16[128,1024]{1,0:T(8,128)(2,1)} %shr.1, bf16[1,394,1024]{2,1,0:T(8,128)(2,1)} %cot.1, ...), custom_call_target="tpu_custom_call" | custom-call | tf_op jit(solution)/shard_map/exchange_compute/pallas_call | solution.py:523
  77.8 0.0 copy-start
  77.8 0.7 copy-done
  78.5 0.0 copy-start.1
  78.5 0.7 copy-done.1
  79.2 0.0 copy-start.2
  79.2 0.6 copy-done.2
  79.8 0.0 copy-start.3
  79.8 0.6 copy-done.3
  80.4 2.2 %write_outputs.1 = (bf16[64,394]{1,0:T(8,128)(2,1)}, f32[64,2048]{1,0:T(8,128)}, f32[128,1024]{1,0:T(8,128)}, f32[1,1024]{1,0:T(1,128)}, f32[1,2048]{1,0:T(1,128...) custom-call(bf16[2,208,128]{2,1,0:T(8,128)(2,1)} %copy-done.2, bf16[16,16,512]{2,1,0:T(8,128)(2,1)} %copy-done, ...), custom_call_target="tpu_custom_call" | custom-call | tf_op jit(solution)/shard_map/write_outputs/pallas_call | solution.py:587
Async XLA Ops:
  77.8 0.7 copy-start
  78.5 0.7 copy-start.1
  79.2 0.6 copy-start.2
  79.8 0.6 copy-start.3

commit v6 on v5

--- a/solution.py
+++ b/solution.py
@@ -14,7 +14,7 @@
 EDGE = 96
 SEAM = 192
 EDGE2 = 288
-PIECES = ((EDGE, SEAM), (SEAM, EDGE2), (0, EDGE), (EDGE2, TOK))
+PIECES = ((0, EDGE), (EDGE2, TOK), (EDGE, SEAM), (SEAM, EDGE2))
 FULL = 416
 D = 1024
 FF = 2048
@@ -151,11 +151,16 @@
         vec_copies[o] = go(remote(
             vec.at[xs[o]], vecs.at[slot_of[o]], vs.at[o - 1], vr.at[o - 1], x=xs[o]
         ))
-    a, b = pl.ds(0, SEAM), pl.ds(SEAM, TOK - SEAM)
-    right_a = go(remote(cot.at[0, a], cots.at[1, a], cs.at[0], cr.at[1, 0], x=xs[1]))
-    left_b = go(remote(cot.at[0, b], cots.at[2, b], cs.at[2], cr.at[2, 1], x=xs[3]))
-    right_b = go(remote(cot.at[0, b], cots.at[1, b], cs.at[1], cr.at[1, 1], x=xs[1]))
-    left_a = go(remote(cot.at[0, a], cots.at[2, a], cs.at[3], cr.at[2, 0], x=xs[3]))
+    right_own, left_own = [], []
+    for i, (lo, hi) in enumerate(((0, EDGE), (EDGE, SEAM), (SEAM, TOK))):
+        piece = pl.ds(lo, hi - lo)
+        right_own.append(remote(cot.at[0, piece], cots.at[1, piece], cs.at[i], cr.at[1, i], x=xs[1]))
+    for i, (lo, hi) in enumerate(((EDGE2, TOK), (SEAM, EDGE2), (0, SEAM))):
+        piece = pl.ds(lo, hi - lo)
+        left_own.append(remote(cot.at[0, piece], cots.at[2, piece], cs.at[3 + i], cr.at[2, i], x=xs[3]))
+    for i in range(3):
+        go(right_own[i])
+        go(left_own[i])
 
     vecs[0] = vec[x]
     here[0].wait()
@@ -186,13 +191,12 @@
     def _(k):
         si[k] = (gained[...] * row(vecs[k], 0)).astype(bf16)
 
-    right_a.wait_recv()
-    left_b.wait_recv()
     fwd = []
     for i, (lo, hi) in enumerate(PIECES):
+        (right_own, left_own)[i % 2][i // 2].wait_recv()
         src, to = ((1, xs[1]), (2, xs[3]))[i % 2]
         piece = pl.ds(lo, hi - lo)
-        fwd.append(go(remote(cots.at[src, piece], cots.at[3, piece], cs.at[4 + i], cr.at[3, i], x=to)))
+        fwd.append(go(remote(cots.at[src, piece], cots.at[3, piece], cs.at[6 + i], cr.at[3, i], x=to)))
     exp_y.wait_recv()
     exp_f = go(remote(w1.at[oy, :, c], w1.at[oy, :, c], es.at[2], er.at[2], c=oc))
     for copy in (shr_c, exp_c, shr_f, exp_f):
@@ -256,11 +260,11 @@
     def _(k):
         @pl.when(k == 1)
         def _():
-            right_b.wait_recv()
+            right_own[2].wait_recv()
 
         @pl.when(k == 2)
         def _():
-            left_a.wait_recv()
+            left_own[2].wait_recv()
 
         every = ((0, TOK),)
         back_proj = back_part(k, every, True)
@@ -334,16 +338,16 @@
     greet(heard.at[3], h=1 - h)
     fwd[0].wait_recv()
     fwd[1].wait_recv()
-    mid, ends = ((EDGE, EDGE2),), ((0, EDGE), (EDGE2, TOK))
-    back_proj = back_part(3, mid, True)
-    expand_part(3, mid, back_proj)
-    norm_part(3, mid, True, back_proj)
+    outer, inner = ((0, EDGE), (EDGE2, TOK)), ((EDGE, EDGE2),)
+    back_proj = back_part(3, outer, True)
+    expand_part(3, outer, back_proj)
+    norm_part(3, outer, True, back_proj)
     told(3, 1)
     for o in (1, 2, 3):
         greet(heard.at[4], x=xs[o])
     fwd[2].wait_recv()
     fwd[3].wait_recv()
-    back_proj = back_part(3, ends, False)
+    back_proj = back_part(3, inner, False)
     for cc in (0, 1):
         for hh in (0, 1):
             for yy in (0, 1):
@@ -351,7 +355,7 @@
                 block = sacc[at : at + 128, SL * hh : SL * hh + SL]
                 pbuf[0, cc, 2 * hh + yy] = block.astype(bf16).reshape(8, 16, SL)
     core_s = core_step(0)
-    expand_part(3, ends, back_proj)
+    expand_part(3, inner, back_proj)
     for cc in (0, 1):
         for hh in (0, 1):
             for yy in (0, 1):
@@ -364,7 +368,7 @@
                         ].astype(bf16)
     core_e = core_step(1)
     ring_s = ring_start(0, core_s)
-    norm_part(3, ends, False, back_proj)
+    norm_part(3, inner, False, back_proj)
     ring_e = ring_start(1, core_e)
 
     vector_copies = []
@@ -523,10 +527,10 @@
     parts = pl.pallas_call(
         kernel,
         out_shape=[
-            V((2, CUT, 128), bf16),
-            V((16, 16, SL), bf16),
-            V((16, 16, SL), bf16),
-            V((16, 1, SL), f32),
+            S((2, CUT, 128), bf16),
+            S((16, 16, SL), bf16),
+            S((16, 16, SL), bf16),
+            S((16, 1, SL), f32),
         ],
         in_specs=[pl.BlockSpec(memory_space=pl.ANY)] * 9,
         out_specs=vmem(4),
@@ -572,7 +576,7 @@
             V((16, 1, SL), f32),
             V((16, 1, SL), f32),
             V((1, SL), f32),
-            dma(10), dma(8), dma(4, 4), dma(3, 2), dma(3, 2), dma(3), dma(3), dma(3), dma(3), dma(3), dma(3),
+            dma(10), dma(10), dma(4, 4), dma(3, 2), dma(3, 2), dma(3), dma(3), dma(3), dma(3), dma(3), dma(3),
             dma(3), dma(3), dma(2, 6), dma(2, 6), dma(5, 8), dma(5, 8), dma(2, 8, 2), dma(2, 8, 2),
             dma(8), dma(8), pltpu.SemaphoreType.DMA, pltpu.SemaphoreType.DMA, dma(3), dma(3), dma(16), dma(16),
             dma(16), dma(16), dma(16), dma(16), pltpu.SemaphoreType.REGULAR((5,)),

time: 82.7 us -> 81.2 us (0.982)
  local copies, waits for them, and re-layouts: 2.63 us -> 0 us
  Pallas kernels: 79.3 us -> 80.5 us
    unnamed x8 -> x0, local copies, waits for them, and re-layouts: 2.63 us -> none
    pallas_call x1, Pallas kernels: 77.1 us -> 78.3 us  [body(): pl.pallas_call(kernel, out_shape=[S((2, CUT, 128), bf16), S((16, 16, SL),...]
where the time goes in v6:
time: 81.2 us; the launch traced here: 81.1 us
  Pallas kernels  80.5 us (99%)
    pallas_call x1, Pallas kernels, body(): pl.pallas_call(kernel, out_shape=[S((2, CUT, 128), bf16), S((16, 16, SL),...  78.3 us
    pallas_call x1, Pallas kernels, body(): pl.pallas_call(finish_kernel, out_shape=[S((64, TOK), bf16), S((64, FF),...  2.17 us

profile of v6, /device:TPU:1, one launch (start us, length us, event | category | flops | bytes accessed | tf_op | source)
XLA Modules:
  0.0 81.1 jit_solution(15732275563881031239)
XLA Ops:
  0.6 78.3 %exchange_compute.1 = (bf16[2,208,128]{2,1,0:T(8,128)(2,1)}, bf16[16,16,512]{2,1,0:T(8,128)(2,1)}, bf16[16,16,512]{2,1,0:T(8,128)(2,1)}, f32[16,1,512]{2,1,0:T(1,128)}) custom-call(bf16[394,1024]{1,0:T(8,128)(2,1)} %trunk.1, bf16[64,2048]{1,0:T(8,128)(2,1)} %exp.1, bf16[128,1024]{1,0:T(8,128)(2,1)} %shr.1, bf16[1,394,1024]{2,1,0:T(8,128)(2,1)} %cot.1, ...), custom_call_target="tpu_custom_call" | custom-call | tf_op jit(solution)/shard_map/exchange_compute/pallas_call | solution.py:527
  78.9 2.2 %write_outputs.1 = (bf16[64,394]{1,0:T(8,128)(2,1)}, f32[64,2048]{1,0:T(8,128)}, f32[128,1024]{1,0:T(8,128)}, f32[1,1024]{1,0:T(1,128)}, f32[1,2048]{1,0:T(1,128...) custom-call(bf16[2,208,128]{2,1,0:T(8,128)(2,1)} %get-tuple-element.20.tf, ...), custom_call_target="tpu_custom_call" | custom-call | tf_op jit(solution)/shard_map/write_outputs/pallas_call | solution.py:591

commit v7 on v6

--- a/solution.py
+++ b/solution.py
@@ -527,10 +527,10 @@
     parts = pl.pallas_call(
         kernel,
         out_shape=[
-            S((2, CUT, 128), bf16),
-            S((16, 16, SL), bf16),
-            S((16, 16, SL), bf16),
-            S((16, 1, SL), f32),
+            V((2, CUT, 128), bf16),
+            V((16, 16, SL), bf16),
+            V((16, 16, SL), bf16),
+            V((16, 1, SL), f32),
         ],
         in_specs=[pl.BlockSpec(memory_space=pl.ANY)] * 9,
         out_specs=vmem(4),
@@ -603,7 +603,7 @@
         in_specs=vmem(4),
         out_specs=vmem(8),
         name="write_outputs",
-    )(*parts)
+    )(*(pltpu.with_memory_space_constraint(part, pltpu.VMEM) for part in parts))
     return tg.T, eg, sg, ing, hg, ag, og, gg.reshape(D)
 
 

time: 81.2 us -> 79 us (0.973)
  Pallas kernels: 80.5 us -> 78.2 us
    pallas_call x1, Pallas kernels: 78.3 us -> 77.1 us  [body(): pl.pallas_call(kernel, out_shape=[V((2, CUT, 128), bf16), V((16, 16, SL),...]
    pallas_call x1, Pallas kernels: 2.17 us -> 1.09 us  [body(): pl.pallas_call(finish_kernel, out_shape=[S((64, TOK), bf16), S((64, FF),...]
where the time goes in v7:
time: 79 us; the launch traced here: 78.9 us
  Pallas kernels  78.2 us (99%)
    pallas_call x1, Pallas kernels, body(): pl.pallas_call(kernel, out_shape=[V((2, CUT, 128), bf16), V((16, 16, SL),...  77.1 us

profile of v7, /device:TPU:1, one launch (start us, length us, event | category | flops | bytes accessed | tf_op | source)
XLA Modules:
  0.0 78.9 jit_solution(16064601060592443882)
XLA Ops:
  0.6 77.1 %exchange_compute.1 = (bf16[2,208,128]{2,1,0:T(8,128)(2,1)S(1)}, bf16[16,16,512]{2,1,0:T(8,128)(2,1)S(1)}, bf16[16,16,512]{2,1,0:T(8,128)(2,1)S(1)}, f32[16,1,512]{2,1,0:T(1,128)S(1)}) custom-call(bf16[394,1024]{1,0:T(8,128)(2,1)} %trunk.1, bf16[64,2048]{1,0:T(8,128)(2,1)} %exp.1, bf16[128,1024]{1,0:T(8,128)(2,1)} %shr.1, bf16[1,394,1024]{2,1,0:T(8,128)(2,1)} %cot.1, ...), custom_call_target="tpu_custom_call" | custom-call | tf_op jit(solution)/shard_map/exchange_compute/pallas_call | solution.py:527
  77.8 1.1 %write_outputs.1 = (bf16[64,394]{1,0:T(8,128)(2,1)}, f32[64,2048]{1,0:T(8,128)}, f32[128,1024]{1,0:T(8,128)}, f32[1,1024]{1,0:T(1,128)}, f32[1,2048]{1,0:T(1,128...) custom-call(bf16[2,208,128]{2,1,0:T(8,128)(2,1)S(1)} %get-tuple-element.20.tf, ...), custom_call_target="tpu_custom_call" | custom-call | tf_op jit(solution)/shard_map/write_outputs/pallas_call | solution.py:591

commit v8 on v7

--- a/solution.py
+++ b/solution.py
@@ -11,14 +11,13 @@
 DP = ("z", "h")
 TOK = 394
 CUT = 208
-EDGE = 96
-SEAM = 192
-EDGE2 = 288
-PIECES = ((0, EDGE), (EDGE2, TOK), (EDGE, SEAM), (SEAM, EDGE2))
+HALF = 256
+PIECES = (0, 512, 256, 768)
 FULL = 416
 D = 1024
 FF = 2048
 SL = 512
+ITEMS = ((0, 0, HALF), (0, HALF, SL), (1, 0, SL))
 
 eps = 1e-06
 coeff = 0.7978845608028654
@@ -65,7 +64,7 @@
 def kernel(
     trunk, exp, shr, cot, gain_in, in_in, hid_in, act_in, out_in,
     tf, sh, ex, dvo,
-    gain, inscale, hidscale, actscale, outscale, tbuf, vec, normed, gained, invs, cots, w1, w2, vecs, si, act, pa, actf, proj, total, sacc, eacc,
+    gain, inscale, hidscale, actscale, outscale, tbuf, vec, normed, gained, invs, cots, w1, w2, vecs, si, act, pa, actf, proj, total, sacc, eacc, half_back,
     pbuf, rbuf, t, rt, q, yb, mix, r, rz, res, tq, tr, sv, svr, gp, gpr, dv, dvr, dvs,
     ls, cs, cr, ws, wr, vs, vr, ss, sr, es, er,
     as_, ar, ys, yr, zs, zr, hs, hr, ts, tr_, fs, fr, bs, br, gs, gr, ds, dr, os_, or_, heard,
@@ -152,12 +151,12 @@
             vec.at[xs[o]], vecs.at[slot_of[o]], vs.at[o - 1], vr.at[o - 1], x=xs[o]
         ))
     right_own, left_own = [], []
-    for i, (lo, hi) in enumerate(((0, EDGE), (EDGE, SEAM), (SEAM, TOK))):
-        piece = pl.ds(lo, hi - lo)
-        right_own.append(remote(cot.at[0, piece], cots.at[1, piece], cs.at[i], cr.at[1, i], x=xs[1]))
-    for i, (lo, hi) in enumerate(((EDGE2, TOK), (SEAM, EDGE2), (0, SEAM))):
-        piece = pl.ds(lo, hi - lo)
-        left_own.append(remote(cot.at[0, piece], cots.at[2, piece], cs.at[3 + i], cr.at[2, i], x=xs[3]))
+    for i, (lo, n) in enumerate(((0, HALF), (256, HALF), (512, SL))):
+        piece = pl.ds(lo, n)
+        right_own.append(remote(cot.at[0, :, piece], cots.at[1, :, piece], cs.at[i], cr.at[1, i], x=xs[1]))
+    for i, (lo, n) in enumerate(((512, HALF), (768, HALF), (0, SL))):
+        piece = pl.ds(lo, n)
+        left_own.append(remote(cot.at[0, :, piece], cots.at[2, :, piece], cs.at[3 + i], cr.at[2, i], x=xs[3]))
     for i in range(3):
         go(right_own[i])
         go(left_own[i])
@@ -192,11 +191,11 @@
         si[k] = (gained[...] * row(vecs[k], 0)).astype(bf16)
 
     fwd = []
-    for i, (lo, hi) in enumerate(PIECES):
+    for i, lo in enumerate(PIECES):
         (right_own, left_own)[i % 2][i // 2].wait_recv()
         src, to = ((1, xs[1]), (2, xs[3]))[i % 2]
-        piece = pl.ds(lo, hi - lo)
-        fwd.append(go(remote(cots.at[src, piece], cots.at[3, piece], cs.at[6 + i], cr.at[3, i], x=to)))
+        piece = pl.ds(lo, HALF)
+        fwd.append(go(remote(cots.at[src, :, piece], cots.at[3, :, piece], cs.at[6 + i], cr.at[3, i], x=to)))
     exp_y.wait_recv()
     exp_f = go(remote(w1.at[oy, :, c], w1.at[oy, :, c], es.at[2], er.at[2], c=oc))
     for copy in (shr_c, exp_c, shr_f, exp_f):
@@ -217,44 +216,37 @@
     told(1, 2)
     tell_z(2)
 
-    def take(ref, k, rows):
-        blocks = [ref[k, lo:hi] for lo, hi in rows]
-        return blocks[0] if len(blocks) == 1 else jnp.concatenate(blocks, axis=0)
-
-    def back_part(k, rows, first):
-        v = vecs[k]
+    def seeds(k, v, at):
         scale_out = row(v, 2)
         second = w2[...].reshape(SL, D)
-        seed = take(cots, k, rows)
-        scaled_cot = (seed.astype(f32) * scale_out).astype(bf16)
-        back = dot(scaled_cot, second, 1, 1)
-        grad_act = jnp.sum(back * take(actf, k, rows), axis=0, keepdims=True)
-        back_hidden = back * take(pa, k, rows)
-        grad_hid = jnp.sum(back_hidden * take(proj, k, rows), axis=0, keepdims=True)
-        back_proj = (back_hidden * v[4:5]).astype(bf16)
-        both = dot(take(act, k, rows), seed, 0, 0)
-        sacc[...] += both * scale_out
-        grad_out = jnp.sum(second.astype(f32) * both, axis=0, keepdims=True)
-        zero = jnp.zeros((2, SL), f32)
-        lines = jnp.concatenate([grad_out[:, :SL], grad_out[:, SL:], grad_hid, grad_act, zero], axis=0)
-        sv[k, 2:8] = lines if first else sv[k, 2:8] + lines
-        return back_proj
-
-    def expand_part(k, rows, back_proj):
-        eacc[...] += dot(take(si, k, rows), back_proj, 0, 0)
-
-    def norm_part(k, rows, first, back_proj):
+        if at is None:
+            return cots[k], scale_out, second
+        cut = lambda m: jnp.concatenate([m[:, at : at + HALF], m[:, at + 512 : at + 512 + HALF]], axis=1)
+        seed = jnp.concatenate([cots[k, :, at : at + HALF], cots[k, :, at + 512 : at + 512 + HALF]], axis=1)
+        return seed, cut(scale_out), cut(second)
+
+    def back_of(seed, scale_out, second):
+        return dot((seed.astype(f32) * scale_out).astype(bf16), second, 1, 1)
+
+    def back_part(k, v, back):
+        grad_act = jnp.sum(back * actf[k], axis=0, keepdims=True)
+        back_hidden = back * pa[k]
+        grad_hid = jnp.sum(back_hidden * proj[k], axis=0, keepdims=True)
+        sv[k, 4:8] = jnp.concatenate([grad_hid, grad_act, jnp.zeros((2, SL), f32)], axis=0)
+        return (back_hidden * v[4:5]).astype(bf16)
+
+    def shrink_part(k, seed, second):
+        both = dot(act[k], seed, 0, 0)
+        return both, jnp.sum(second.astype(f32) * both, axis=0, keepdims=True)
+
+    def expand_part(k, back_proj):
+        eacc[...] += dot(si[k], back_proj, 0, 0)
+
+    def norm_part(k, v, back_proj):
         back_norm = dot(back_proj, w1[...].reshape(D, SL), 1, 1)
-        share = back_norm * row(vecs[k], 0)
-        grad_in = 0.0
-        at = 0
-        for lo, hi in rows:
-            end = at + hi - lo
-            grad_in = grad_in + jnp.sum(back_norm[at:end] * gained[lo:hi], axis=0, keepdims=True)
-            total[lo:hi] += share[at:end]
-            at = end
-        lines = jnp.concatenate([grad_in[:, :SL], grad_in[:, SL:]], axis=0)
-        sv[k, 0:2] = lines if first else sv[k, 0:2] + lines
+        grad_in = jnp.sum(back_norm * gained[...], axis=0, keepdims=True)
+        total[...] += back_norm * row(v, 0)
+        sv[k, 0:2] = jnp.concatenate([grad_in[:, :SL], grad_in[:, SL:]], axis=0)
 
     @pl.loop(0, 3)
     def _(k):
@@ -266,48 +258,64 @@
         def _():
             left_own[2].wait_recv()
 
-        every = ((0, TOK),)
-        back_proj = back_part(k, every, True)
-        expand_part(k, every, back_proj)
-        norm_part(k, every, True, back_proj)
+        v = vecs[k]
+        seed, scale_out, second = seeds(k, v, None)
+        back_proj = back_part(k, v, back_of(seed, scale_out, second))
+        both, grad_out = shrink_part(k, seed, second)
+        sacc[...] += both * scale_out
+        sv[k, 2:4] = jnp.concatenate([grad_out[:, :SL], grad_out[:, SL:]], axis=0)
+        expand_part(k, back_proj)
+        norm_part(k, v, back_proj)
 
     right, left, far = (lax.rem(place + o, 4) for o in (1, 3, 2))
     to_right = dict(y=lax.rem(right, 2), h=right // 2)
     to_left = dict(y=lax.rem(left, 2), h=left // 2)
     top, low = pl.ds(0, 4), pl.ds(4, 4)
 
-    def core_step(i):
-        return go(remote(pbuf.at[i, oc], rbuf.at[i], as_.at[i], ar.at[i], c=oc))
-
-    def ring_start(i, copy):
+    def lanes(it):
+        i, lo, hi = ITEMS[it]
+        return i, slice(lo, hi), pl.ds(lo, hi - lo)
+
+    def core_step(it):
+        i, _, l = lanes(it)
+        return go(remote(pbuf.at[i, oc, :, :, :, l], rbuf.at[i, :, :, :, l], as_.at[it], ar.at[it], c=oc))
+
+    def ring_start(it, copy):
+        i, v, l = lanes(it)
         copy.wait_recv()
-        q[i] = added(pbuf[i, c], rbuf[i]).astype(bf16)
+        q[i, :, :, :, v] = added(pbuf[i, c, :, :, :, v], rbuf[i, :, :, :, v]).astype(bf16)
         return [
-            go(remote(q.at[i, far, top], yb.at[i, 0], ys.at[i, 0], yr.at[i, 0], **to_right)),
-            go(remote(q.at[i, far, low], yb.at[i, 1], ys.at[i, 1], yr.at[i, 1], **to_left)),
-            go(remote(q.at[i, right, low], yb.at[i, 2], ys.at[i, 2], yr.at[i, 2], **to_right)),
-            go(remote(q.at[i, left, top], yb.at[i, 3], ys.at[i, 3], yr.at[i, 3], **to_left)),
+            go(remote(q.at[i, far, top, :, l], yb.at[i, 0, :, :, l], ys.at[it, 0], yr.at[it, 0], **to_right)),
+            go(remote(q.at[i, far, low, :, l], yb.at[i, 1, :, :, l], ys.at[it, 1], yr.at[it, 1], **to_left)),
+            go(remote(q.at[i, right, low, :, l], yb.at[i, 2, :, :, l], ys.at[it, 2], yr.at[it, 2], **to_right)),
+            go(remote(q.at[i, left, top, :, l], yb.at[i, 3, :, :, l], ys.at[it, 3], yr.at[it, 3], **to_left)),
         ]
 
-    def ring_pass(i, copies):
+    def ring_pass(it, copies):
+        i, v, l = lanes(it)
         copies[0].wait_recv()
-        mix[i, 0] = added(q[i, right, 0:4], yb[i, 0]).astype(bf16)
-        copies.append(go(remote(mix.at[i, 0], yb.at[i, 4], ys.at[i, 4], yr.at[i, 4], **to_right)))
+        mix[i, 0, :, :, v] = added(q[i, right, 0:4, :, v], yb[i, 0, :, :, v]).astype(bf16)
+        copies.append(go(remote(
+            mix.at[i, 0, :, :, l], yb.at[i, 4, :, :, l], ys.at[it, 4], yr.at[it, 4], **to_right
+        )))
         copies[1].wait_recv()
-        mix[i, 1] = added(q[i, left, 4:8], yb[i, 1]).astype(bf16)
-        copies.append(go(remote(mix.at[i, 1], yb.at[i, 5], ys.at[i, 5], yr.at[i, 5], **to_left)))
-
-    def deep_start(i, copies):
+        mix[i, 1, :, :, v] = added(q[i, left, 4:8, :, v], yb[i, 1, :, :, v]).astype(bf16)
+        copies.append(go(remote(
+            mix.at[i, 1, :, :, l], yb.at[i, 5, :, :, l], ys.at[it, 5], yr.at[it, 5], **to_left
+        )))
+
+    def deep_start(it, copies):
+        i, v, l = lanes(it)
         for copy in copies[2:]:
             copy.wait_recv()
-        r[i, 0:4] = added(q[i, place, 0:4], yb[i, 3], yb[i, 4]).astype(bf16)
-        r[i, 4:8] = added(q[i, place, 4:8], yb[i, 2], yb[i, 5]).astype(bf16)
+        r[i, 0:4, :, v] = added(q[i, place, 0:4, :, v], yb[i, 3, :, :, v], yb[i, 4, :, :, v]).astype(bf16)
+        r[i, 4:8, :, v] = added(q[i, place, 4:8, :, v], yb[i, 2, :, :, v], yb[i, 5, :, :, v]).astype(bf16)
         out = []
         if i == 0:
             for o in (4, 3, 5, 2, 6, 1, 7):
                 e = lax.rem(z + o, 8)
-                out.append(go(remote(r.at[0, e], rz.at[0, z], zs.at[0, o], zr.at[0, o], z=e)))
-            rz[0, z] = r[0, z]
+                out.append(go(remote(r.at[0, e, :, l], rz.at[0, z, :, l], zs.at[it, o], zr.at[it, o], z=e)))
+            rz[0, z, :, v] = r[0, z, :, v]
             return out
         mine = pl.ds(pl.multiple_of(128 * x, 128), 128)
         for o in (4, 3, 5, 2, 6, 1, 7, 0):
@@ -316,17 +324,18 @@
                 if o or xo:
                     block = pl.ds(pl.multiple_of(128 * xs[xo], 128), 128)
                     out.append(go(remote(
-                        r.at[1, e, :, block], rz.at[1, z, :, mine], zs.at[1 + xo, o], zr.at[1 + xo, o],
+                        r.at[1, e, :, block], rz.at[1, z, :, mine], zs.at[2 + xo, o], zr.at[2 + xo, o],
                         z=e, x=xs[xo],
                     )))
         rz[1, z, :, mine] = r[1, z, :, mine]
         return out
 
-    def deep_sum(i, copies):
+    def deep_sum(it, copies):
+        i, v, _ = lanes(it)
         for copy in copies:
             copy.wait_recv()
-        done = added(*(rz[i, e] for e in range(8))).astype(bf16)
-        res[i] = done
+        done = added(*(rz[i, e, :, v] for e in range(8))).astype(bf16)
+        res[i, :, v] = done
         return done
 
     peers = []
@@ -334,28 +343,36 @@
         e = lax.rem(me + o, 16)
         peers.append((o, dict(z=e // 2, h=lax.rem(e, 2))))
 
+    def shrink_blocks(it, both, scale_out):
+        _, lo, hi = ITEMS[it]
+        for cc in (0, 1):
+            for hh in (0, 1):
+                for yy in (0, 1):
+                    at = (yy * 2 + cc) * 128
+                    new = both[at : at + 128, HALF * hh : HALF * hh + HALF] * scale_out[:, HALF * hh : HALF * hh + HALF]
+                    block = sacc[at : at + 128, SL * hh + lo : SL * hh + hi] + new
+                    pbuf[0, cc, 2 * hh + yy, :, :, lo:hi] = block.astype(bf16).reshape(8, 16, HALF)
+
     told(2, 2)
     greet(heard.at[3], h=1 - h)
+    v = vecs[3]
     fwd[0].wait_recv()
     fwd[1].wait_recv()
-    outer, inner = ((0, EDGE), (EDGE2, TOK)), ((EDGE, EDGE2),)
-    back_proj = back_part(3, outer, True)
-    expand_part(3, outer, back_proj)
-    norm_part(3, outer, True, back_proj)
+    seed, scale_out, second = seeds(3, v, 0)
+    both, grad_first = shrink_part(3, seed, second)
+    shrink_blocks(0, both, scale_out)
+    core_s = core_step(0)
+    half_back[...] = back_of(seed, scale_out, second)
     told(3, 1)
     for o in (1, 2, 3):
         greet(heard.at[4], x=xs[o])
+    ring_s = ring_start(0, core_s)
+
     fwd[2].wait_recv()
     fwd[3].wait_recv()
-    back_proj = back_part(3, inner, False)
-    for cc in (0, 1):
-        for hh in (0, 1):
-            for yy in (0, 1):
-                at = (yy * 2 + cc) * 128
-                block = sacc[at : at + 128, SL * hh : SL * hh + SL]
-                pbuf[0, cc, 2 * hh + yy] = block.astype(bf16).reshape(8, 16, SL)
-    core_s = core_step(0)
-    expand_part(3, inner, back_proj)
+    seed, scale_out, second = seeds(3, v, HALF)
+    back_proj = back_part(3, v, half_back[...] + back_of(seed, scale_out, second))
+    expand_part(3, back_proj)
     for cc in (0, 1):
         for hh in (0, 1):
             for yy in (0, 1):
@@ -366,10 +383,21 @@
                         pbuf[1, cc, 2 * hh + yy, zz, :, 128 * xx : 128 * xx + 128] = eacc[
                             top_row : top_row + 16, lane : lane + 128
                         ].astype(bf16)
-    core_e = core_step(1)
-    ring_s = ring_start(0, core_s)
-    norm_part(3, inner, False, back_proj)
-    ring_e = ring_start(1, core_e)
+    core_e = core_step(2)
+    ring_pass(0, ring_s)
+    both, grad_last = shrink_part(3, seed, second)
+    shrink_blocks(1, both, scale_out)
+    core_l = core_step(1)
+    ring_e = ring_start(2, core_e)
+    norm_part(3, v, back_proj)
+    ring_l = ring_start(1, core_l)
+    sv[3, 2:4] = jnp.concatenate(
+        [
+            jnp.concatenate([grad_first[:, :HALF], grad_last[:, :HALF]], axis=1),
+            jnp.concatenate([grad_first[:, HALF:], grad_last[:, HALF:]], axis=1),
+        ],
+        axis=0,
+    )
 
     vector_copies = []
     for slot, xo in ((1, 3), (2, 1), (3, 2)):
@@ -391,13 +419,14 @@
     t[0] = term[:CUT]
     t[1, : TOK - CUT] = term[CUT:]
     t[1, TOK - CUT :] = jnp.zeros((FULL - TOK, D), bf16)
-    core_t = go(remote(t.at[oc], rt, as_.at[2], ar.at[2], c=oc))
-
-    ring_pass(0, ring_s)
-    ring_pass(1, ring_e)
+    core_t = go(remote(t.at[oc], rt, as_.at[3], ar.at[3], c=oc))
+
+    ring_pass(2, ring_e)
+    ring_pass(1, ring_l)
     told(4, 3)
     deep_s = deep_start(0, ring_s)
-    deep_e = deep_start(1, ring_e)
+    deep_e = deep_start(2, ring_e)
+    deep_l = deep_start(1, ring_l)
 
     core_t.wait_recv()
     joint = added(t[c], rt[...]).astype(bf16)
@@ -433,35 +462,40 @@
 
     outs = (sh, ex)
 
-    def spread(i):
+    def spread(it):
+        i, _, l = lanes(it)
         copies = {}
         for o in (2, 6, 1, 7, 0):
             e = lax.rem(z + o, 8)
             for ho in (0, 1):
                 if o or ho:
                     copies[o, ho] = go(remote(
-                        res.at[i], outs[i].at[me], hs.at[i, o, ho], hr.at[i, o, ho],
+                        res.at[i, :, l], outs[i].at[me, :, l], hs.at[it, o, ho], hr.at[it, o, ho],
                         z=e, h=1 - h if ho else h,
                     ))
         return copies
 
-    def relay(i, copies):
+    def relay(it, copies):
+        i, _, l = lanes(it)
         for o, further in ((2, (4, 3)), (6, (5,))):
             for ho in (0, 1):
                 copies[o, ho].wait_recv()
-                place = lax.rem(z + 8 - o, 8) * 2 + (1 - h if ho else h)
+                part = outs[i].at[lax.rem(z + 8 - o, 8) * 2 + (1 - h if ho else h), :, l]
                 for far_o in further:
                     copies[far_o, ho] = go(remote(
-                        outs[i].at[place], outs[i].at[place], hs.at[i, far_o, ho], hr.at[i, far_o, ho],
+                        part, part, hs.at[it, far_o, ho], hr.at[it, far_o, ho],
                         z=lax.rem(z + far_o - o + 8, 8),
                     ))
 
     done = deep_sum(0, deep_s)
     spread_s = spread(0)
-    sh[me] = done
-    done = deep_sum(1, deep_e)
-    spread_e = spread(1)
+    sh[me, :, :HALF] = done
+    done = deep_sum(2, deep_e)
+    spread_e = spread(2)
     ex[me] = done
+    done = deep_sum(1, deep_l)
+    spread_l = spread(1)
+    sh[me, :, HALF:] = done
 
     for copy in tiles:
         copy.wait_recv()
@@ -480,11 +514,12 @@
     dvo[me] = line
 
     relay(0, spread_s)
-    relay(1, spread_e)
+    relay(2, spread_e)
+    relay(1, spread_l)
 
     for copy in [finish] + lines:
         copy.wait_recv()
-    for copies in (spread_s, spread_e):
+    for copies in (spread_s, spread_e, spread_l):
         for (o, ho), copy in copies.items():
             if o not in (2, 6):
                 copy.wait_recv()
@@ -557,6 +592,7 @@
             V((TOK, D), f32),
             V((SL, D), f32),
             V((D, SL), f32),
+            V((TOK, SL), f32),
             V((2, 2, 4, 8, 16, SL), bf16),
             V((2, 4, 8, 16, SL), bf16),
             V((2, CUT, D), bf16),
@@ -577,7 +613,7 @@
             V((16, 1, SL), f32),
             V((1, SL), f32),
             dma(10), dma(10), dma(4, 4), dma(3, 2), dma(3, 2), dma(3), dma(3), dma(3), dma(3), dma(3), dma(3),
-            dma(3), dma(3), dma(2, 6), dma(2, 6), dma(5, 8), dma(5, 8), dma(2, 8, 2), dma(2, 8, 2),
+            dma(4), dma(4), dma(3, 6), dma(3, 6), dma(6, 8), dma(6, 8), dma(3, 8, 2), dma(3, 8, 2),
             dma(8), dma(8), pltpu.SemaphoreType.DMA, pltpu.SemaphoreType.DMA, dma(3), dma(3), dma(16), dma(16),
             dma(16), dma(16), dma(16), dma(16), pltpu.SemaphoreType.REGULAR((5,)),
         ],

time: 79 us -> 77.4 us (0.980)
  Pallas kernels: 78.2 us -> 76.6 us
    pallas_call x1, Pallas kernels: 77.1 us -> 75.5 us  [body(): pl.pallas_call(kernel, out_shape=[V((2, CUT, 128), bf16), V((16, 16, SL),...]
where the time goes in v8:
time: 77.4 us; the launch traced here: 77.2 us
  Pallas kernels  76.6 us (99%)
    pallas_call x1, Pallas kernels, body(): pl.pallas_call(kernel, out_shape=[V((2, CUT, 128), bf16), V((16, 16, SL),...  75.5 us

profile of v8, /device:TPU:1, one launch (start us, length us, event | category | flops | bytes accessed | tf_op | source)
XLA Modules:
  0.0 77.2 jit_solution(14997581139804251341)
XLA Ops:
  0.6 75.5 %exchange_compute.1 = (bf16[2,208,128]{2,1,0:T(8,128)(2,1)S(1)}, bf16[16,16,512]{2,1,0:T(8,128)(2,1)S(1)}, bf16[16,16,512]{2,1,0:T(8,128)(2,1)S(1)}, f32[16,1,512]{2,1,0:T(1,128)S(1)}) custom-call(bf16[394,1024]{1,0:T(8,128)(2,1)} %trunk.1, bf16[64,2048]{1,0:T(8,128)(2,1)} %exp.1, bf16[128,1024]{1,0:T(8,128)(2,1)} %shr.1, bf16[1,394,1024]{2,1,0:T(8,128)(2,1)} %cot.1, ...), custom_call_target="tpu_custom_call" | custom-call | tf_op jit(solution)/shard_map/exchange_compute/pallas_call | solution.py:562
  76.1 1.1 %write_outputs.1 = (bf16[64,394]{1,0:T(8,128)(2,1)}, f32[64,2048]{1,0:T(8,128)}, f32[128,1024]{1,0:T(8,128)}, f32[1,1024]{1,0:T(1,128)}, f32[1,2048]{1,0:T(1,128...) custom-call(bf16[2,208,128]{2,1,0:T(8,128)(2,1)S(1)} %get-tuple-element.20.tf, ...), custom_call_target="tpu_custom_call" | custom-call | tf_op jit(solution)/shard_map/write_outputs/pallas_call | solution.py:627

commit v9 on v8

--- a/solution.py
+++ b/solution.py
@@ -127,14 +127,18 @@
 
     slot_of = {1: 1, 3: 2, 2: 3}
     vec_copies, exp_copies = {}, {}
+    rows_here = pl.ds(pl.multiple_of(32 * h, 32), 32)
+    rows_there = pl.ds(pl.multiple_of(32 * (1 - h), 32), 32)
+    wide_here = pl.ds(pl.multiple_of(64 * h, 64), 64)
     for o in (1, 3, 2):
         for half in (0, 1):
             exp_copies[o, half] = go(remote(
-                exp.at[:, pl.ds(pl.multiple_of(1024 * half + 256 * xs[o], 256), 256)],
-                w1.at[y, x, c, :, pl.ds(256 * half, 256)],
+                exp.at[rows_here, pl.ds(pl.multiple_of(1024 * half + 256 * xs[o], 256), 256)],
+                w1.at[y, x, c, rows_here, pl.ds(256 * half, 256)],
                 ws.at[o - 1, half], wr.at[o - 1, half], x=xs[o],
             ))
-    shr_y = go(remote(shr, w2.at[y, c], ss.at[0], sr.at[0], y=oy))
+    shr_y = go(remote(shr.at[wide_here], w2.at[y, c, wide_here], ss.at[0], sr.at[0], y=oy))
+    shr_n = go(remote(shr.at[wide_here], w2.at[y, c, wide_here], ss.at[3], sr.at[3], y=oy, h=1 - h))
     shr_c = go(remote(shr, w2.at[y, c], ss.at[1], sr.at[1], c=oc))
     for copy in lines:
         copy.wait()
@@ -179,9 +183,16 @@
     for o in (1, 3, 2):
         exp_copies[o, 0].wait_recv()
         exp_copies[o, 1].wait_recv()
-    exp_y = go(remote(w1.at[y, :, c], w1.at[y, :, c], es.at[0], er.at[0], y=oy))
-    exp_c = go(remote(w1.at[y, :, c], w1.at[y, :, c], es.at[1], er.at[1], c=oc))
+    exp_h = []
+    for o in (1, 2, 3):
+        part = w1.at[y, xs[o], c, rows_here]
+        exp_h.append(go(remote(part, part, es.at[o - 1], er.at[o - 1], h=1 - h)))
+    part = w1.at[y, :, c, rows_here]
+    exp_y = go(remote(part, part, es.at[3], er.at[3], y=oy))
+    exp_n = go(remote(part, part, es.at[4], er.at[4], y=oy, h=1 - h))
+    exp_c = go(remote(part, part, es.at[5], er.at[5], c=oc))
     shr_y.wait_recv()
+    shr_n.wait_recv()
     shr_f = go(remote(w2.at[oy, c], w2.at[oy, c], ss.at[2], sr.at[2], c=oc))
     for o in (1, 3, 2):
         vec_copies[o].wait_recv()
@@ -189,6 +200,11 @@
     @pl.loop(0, 4)
     def _(k):
         si[k] = (gained[...] * row(vecs[k], 0)).astype(bf16)
+
+    for copy in exp_h:
+        copy.wait_recv()
+    part = w1.at[y, :, c, rows_there]
+    exp_d = go(remote(part, part, es.at[6], er.at[6], c=oc))
 
     fwd = []
     for i, lo in enumerate(PIECES):
@@ -197,8 +213,9 @@
         piece = pl.ds(lo, HALF)
         fwd.append(go(remote(cots.at[src, :, piece], cots.at[3, :, piece], cs.at[6 + i], cr.at[3, i], x=to)))
     exp_y.wait_recv()
-    exp_f = go(remote(w1.at[oy, :, c], w1.at[oy, :, c], es.at[2], er.at[2], c=oc))
-    for copy in (shr_c, exp_c, shr_f, exp_f):
+    exp_n.wait_recv()
+    exp_f = go(remote(w1.at[oy, :, c], w1.at[oy, :, c], es.at[7], er.at[7], c=oc))
+    for copy in (shr_c, exp_c, exp_d, shr_f, exp_f):
         copy.wait_recv()
     told(0, 2)
     tell_z(1)
@@ -228,12 +245,13 @@
     def back_of(seed, scale_out, second):
         return dot((seed.astype(f32) * scale_out).astype(bf16), second, 1, 1)
 
-    def back_part(k, v, back):
+    def back_part(v, back, k):
+        return (back * pa[k] * v[4:5]).astype(bf16)
+
+    def back_sums(back, k):
         grad_act = jnp.sum(back * actf[k], axis=0, keepdims=True)
-        back_hidden = back * pa[k]
-        grad_hid = jnp.sum(back_hidden * proj[k], axis=0, keepdims=True)
+        grad_hid = jnp.sum(back * pa[k] * proj[k], axis=0, keepdims=True)
         sv[k, 4:8] = jnp.concatenate([grad_hid, grad_act, jnp.zeros((2, SL), f32)], axis=0)
-        return (back_hidden * v[4:5]).astype(bf16)
 
     def shrink_part(k, seed, second):
         both = dot(act[k], seed, 0, 0)
@@ -260,7 +278,9 @@
 
         v = vecs[k]
         seed, scale_out, second = seeds(k, v, None)
-        back_proj = back_part(k, v, back_of(seed, scale_out, second))
+        back = back_of(seed, scale_out, second)
+        back_proj = back_part(v, back, k)
+        back_sums(back, k)
         both, grad_out = shrink_part(k, seed, second)
         sacc[...] += both * scale_out
         sv[k, 2:4] = jnp.concatenate([grad_out[:, :SL], grad_out[:, SL:]], axis=0)
@@ -371,7 +391,8 @@
     fwd[2].wait_recv()
     fwd[3].wait_recv()
     seed, scale_out, second = seeds(3, v, HALF)
-    back_proj = back_part(3, v, half_back[...] + back_of(seed, scale_out, second))
+    back = half_back[...] + back_of(seed, scale_out, second)
+    back_proj = back_part(v, back, 3)
     expand_part(3, back_proj)
     for cc in (0, 1):
         for hh in (0, 1):
@@ -389,6 +410,7 @@
     shrink_blocks(1, both, scale_out)
     core_l = core_step(1)
     ring_e = ring_start(2, core_e)
+    back_sums(back, 3)
     norm_part(3, v, back_proj)
     ring_l = ring_start(1, core_l)
     sv[3, 2:4] = jnp.concatenate(
@@ -612,7 +634,7 @@
             V((16, 1, SL), f32),
             V((16, 1, SL), f32),
             V((1, SL), f32),
-            dma(10), dma(10), dma(4, 4), dma(3, 2), dma(3, 2), dma(3), dma(3), dma(3), dma(3), dma(3), dma(3),
+            dma(10), dma(10), dma(4, 4), dma(3, 2), dma(3, 2), dma(3), dma(3), dma(4), dma(4), dma(8), dma(8),
             dma(4), dma(4), dma(3, 6), dma(3, 6), dma(6, 8), dma(6, 8), dma(3, 8, 2), dma(3, 8, 2),
             dma(8), dma(8), pltpu.SemaphoreType.DMA, pltpu.SemaphoreType.DMA, dma(3), dma(3), dma(16), dma(16),
             dma(16), dma(16), dma(16), dma(16), pltpu.SemaphoreType.REGULAR((5,)),

time: 77.4 us -> 75.6 us (0.977)
  Pallas kernels: 76.6 us -> 74.8 us
    pallas_call x1, Pallas kernels: 75.5 us -> 73.8 us  [body(): pl.pallas_call(kernel, out_shape=[V((2, CUT, 128), bf16), V((16, 16, SL),...]
where the time goes in v9:
time: 75.6 us; the launch traced here: 75.5 us
  Pallas kernels  74.8 us (99%)
    pallas_call x1, Pallas kernels, body(): pl.pallas_call(kernel, out_shape=[V((2, CUT, 128), bf16), V((16, 16, SL),...  73.8 us

profile of v9, /device:TPU:1, one launch (start us, length us, event | category | flops | bytes accessed | tf_op | source)
XLA Modules:
  0.0 75.5 jit_solution(13118957535781168531)
XLA Ops:
  0.6 73.8 %exchange_compute.1 = (bf16[2,208,128]{2,1,0:T(8,128)(2,1)S(1)}, bf16[16,16,512]{2,1,0:T(8,128)(2,1)S(1)}, bf16[16,16,512]{2,1,0:T(8,128)(2,1)S(1)}, f32[16,1,512]{2,1,0:T(1,128)S(1)}) custom-call(bf16[394,1024]{1,0:T(8,128)(2,1)} %trunk.1, bf16[64,2048]{1,0:T(8,128)(2,1)} %exp.1, bf16[128,1024]{1,0:T(8,128)(2,1)} %shr.1, bf16[1,394,1024]{2,1,0:T(8,128)(2,1)} %cot.1, ...), custom_call_target="tpu_custom_call" | custom-call | tf_op jit(solution)/shard_map/exchange_compute/pallas_call | solution.py:584
  74.4 1.1 %write_outputs.1 = (bf16[64,394]{1,0:T(8,128)(2,1)}, f32[64,2048]{1,0:T(8,128)}, f32[128,1024]{1,0:T(8,128)}, f32[1,1024]{1,0:T(1,128)}, f32[1,2048]{1,0:T(1,128...) custom-call(bf16[2,208,128]{2,1,0:T(8,128)(2,1)S(1)} %get-tuple-element.20.tf, ...), custom_call_target="tpu_custom_call" | custom-call | tf_op jit(solution)/shard_map/write_outputs/pallas_call | solution.py:649

commit v10 on v9

--- a/solution.py
+++ b/solution.py
@@ -413,6 +413,8 @@
     back_sums(back, 3)
     norm_part(3, v, back_proj)
     ring_l = ring_start(1, core_l)
+    told(4, 3)
+    deep_s = deep_start(0, ring_s)
     sv[3, 2:4] = jnp.concatenate(
         [
             jnp.concatenate([grad_first[:, :HALF], grad_last[:, :HALF]], axis=1),
@@ -420,6 +422,33 @@
         ],
         axis=0,
     )
+
+    outs = (sh, ex)
+
+    def spread(it):
+        i, _, l = lanes(it)
+        copies = {}
+        for o in (2, 6, 1, 7, 0):
+            e = lax.rem(z + o, 8)
+            for ho in (0, 1):
+                if o or ho:
+                    copies[o, ho] = go(remote(
+                        res.at[i, :, l], outs[i].at[me, :, l], hs.at[it, o, ho], hr.at[it, o, ho],
+                        z=e, h=1 - h if ho else h,
+                    ))
+        return copies
+
+    def relay(it, copies):
+        i, _, l = lanes(it)
+        for o, further in ((2, (4, 3)), (6, (5,))):
+            for ho in (0, 1):
+                copies[o, ho].wait_recv()
+                part = outs[i].at[lax.rem(z + 8 - o, 8) * 2 + (1 - h if ho else h), :, l]
+                for far_o in further:
+                    copies[far_o, ho] = go(remote(
+                        part, part, hs.at[it, far_o, ho], hr.at[it, far_o, ho],
+                        z=lax.rem(z + far_o - o + 8, 8),
+                    ))
 
     vector_copies = []
     for slot, xo in ((1, 3), (2, 1), (3, 2)):
@@ -445,8 +474,6 @@
 
     ring_pass(2, ring_e)
     ring_pass(1, ring_l)
-    told(4, 3)
-    deep_s = deep_start(0, ring_s)
     deep_e = deep_start(2, ring_e)
     deep_l = deep_start(1, ring_l)
 
@@ -460,6 +487,10 @@
         ty, tx = oy if yo else y, xs[xo]
         tiles.append(go(remote(tq.at[ty * 4 + tx], tr.at[chip], ts.at[g], tr_.at[g], y=ty, x=tx)))
     tr[chip] = tq[chip]
+
+    done = deep_sum(0, deep_s)
+    spread_s = spread(0)
+    sh[me, :, :HALF] = done
 
     for copy in vector_copies + gains:
         copy.wait_recv()
@@ -482,48 +513,12 @@
         small.append(go(remote(dv.at[e], dvr.at[me], ds.at[o], dr.at[o], **where)))
     dvr[me] = dv[me]
 
-    outs = (sh, ex)
-
-    def spread(it):
-        i, _, l = lanes(it)
-        copies = {}
-        for o in (2, 6, 1, 7, 0):
-            e = lax.rem(z + o, 8)
-            for ho in (0, 1):
-                if o or ho:
-                    copies[o, ho] = go(remote(
-                        res.at[i, :, l], outs[i].at[me, :, l], hs.at[it, o, ho], hr.at[it, o, ho],
-                        z=e, h=1 - h if ho else h,
-                    ))
-        return copies
-
-    def relay(it, copies):
-        i, _, l = lanes(it)
-        for o, further in ((2, (4, 3)), (6, (5,))):
-            for ho in (0, 1):
-                copies[o, ho].wait_recv()
-                part = outs[i].at[lax.rem(z + 8 - o, 8) * 2 + (1 - h if ho else h), :, l]
-                for far_o in further:
-                    copies[far_o, ho] = go(remote(
-                        part, part, hs.at[it, far_o, ho], hr.at[it, far_o, ho],
-                        z=lax.rem(z + far_o - o + 8, 8),
-                    ))
-
-    done = deep_sum(0, deep_s)
-    spread_s = spread(0)
-    sh[me, :, :HALF] = done
     done = deep_sum(2, deep_e)
     spread_e = spread(2)
     ex[me] = done
     done = deep_sum(1, deep_l)
     spread_l = spread(1)
     sh[me, :, HALF:] = done
-
-    for copy in tiles:
-        copy.wait_recv()
-    tf[c] = added(*(tr[g] for g in range(8))).astype(bf16)
-    finish = go(remote(tf.at[c], tf.at[c], fs, fr, c=oc))
-
     for copy in small:
         copy.wait_recv()
     line = dvr[0]
@@ -534,8 +529,13 @@
     for o, where in peers:
         lines.append(go(remote(dvs, dvo.at[me], os_.at[o], or_.at[o], **where)))
     dvo[me] = line
-
     relay(0, spread_s)
+
+    for copy in tiles:
+        copy.wait_recv()
+    tf[c] = added(*(tr[g] for g in range(8))).astype(bf16)
+    finish = go(remote(tf.at[c], tf.at[c], fs, fr, c=oc))
+
     relay(2, spread_e)
     relay(1, spread_l)
 

time: 75.6 us -> 74.4 us (0.984)
  Pallas kernels: 74.8 us -> 73.2 us
    pallas_call x1, Pallas kernels: 73.8 us -> 72.1 us  [body(): pl.pallas_call(kernel, out_shape=[V((2, CUT, 128), bf16), V((16, 16, SL),...]
where the time goes in v10:
time: 74.4 us; the launch traced here: 73.8 us
  Pallas kernels  73.2 us (98%)
    pallas_call x1, Pallas kernels, body(): pl.pallas_call(kernel, out_shape=[V((2, CUT, 128), bf16), V((16, 16, SL),...  72.1 us

profile of v10, /device:TPU:1, one launch (start us, length us, event | category | flops | bytes accessed | tf_op | source)
XLA Modules:
  0.0 73.8 jit_solution(1405902091864176099)
XLA Ops:
  0.6 72.1 %exchange_compute.1 = (bf16[2,208,128]{2,1,0:T(8,128)(2,1)S(1)}, bf16[16,16,512]{2,1,0:T(8,128)(2,1)S(1)}, bf16[16,16,512]{2,1,0:T(8,128)(2,1)S(1)}, f32[16,1,512]{2,1,0:T(1,128)S(1)}) custom-call(bf16[394,1024]{1,0:T(8,128)(2,1)} %trunk.1, bf16[64,2048]{1,0:T(8,128)(2,1)} %exp.1, bf16[128,1024]{1,0:T(8,128)(2,1)} %shr.1, bf16[1,394,1024]{2,1,0:T(8,128)(2,1)} %cot.1, ...), custom_call_target="tpu_custom_call" | custom-call | tf_op jit(solution)/shard_map/exchange_compute/pallas_call | solution.py:584
  72.7 1.1 %write_outputs.1 = (bf16[64,394]{1,0:T(8,128)(2,1)}, f32[64,2048]{1,0:T(8,128)}, f32[128,1024]{1,0:T(8,128)}, f32[1,1024]{1,0:T(1,128)}, f32[1,2048]{1,0:T(1,128...) custom-call(bf16[2,208,128]{2,1,0:T(8,128)(2,1)S(1)} %get-tuple-element.20.tf, ...), custom_call_target="tpu_custom_call" | custom-call | tf_op jit(solution)/shard_map/write_outputs/pallas_call | solution.py:649

commit v11 on v10

--- a/solution.py
+++ b/solution.py
@@ -81,6 +81,11 @@
         copy.start()
         sent.append(copy)
         return copy
+
+    def drain(n):
+        for copy in sent[:n]:
+            copy.wait_send()
+        del sent[:n]
 
     barrier = pltpu.get_barrier_semaphore()
 
@@ -475,6 +480,7 @@
     ring_pass(2, ring_e)
     ring_pass(1, ring_l)
     deep_e = deep_start(2, ring_e)
+    first_sends = len(sent)
     deep_l = deep_start(1, ring_l)
 
     core_t.wait_recv()
@@ -513,6 +519,8 @@
         small.append(go(remote(dv.at[e], dvr.at[me], ds.at[o], dr.at[o], **where)))
     dvr[me] = dv[me]
 
+    drain(first_sends)
+    other_sends = len(sent)
     done = deep_sum(2, deep_e)
     spread_e = spread(2)
     ex[me] = done
@@ -536,6 +544,7 @@
     tf[c] = added(*(tr[g] for g in range(8))).astype(bf16)
     finish = go(remote(tf.at[c], tf.at[c], fs, fr, c=oc))
 
+    drain(other_sends)
     relay(2, spread_e)
     relay(1, spread_l)
 
@@ -546,8 +555,7 @@
             if o not in (2, 6):
                 copy.wait_recv()
 
-    for copy in sent:
-        copy.wait_send()
+    drain(len(sent))
 
 
 def finish_kernel(tf, sh, ex, dvo, tg, eg, sg, ing, hg, ag, og, gg):

time: 74.4 us -> 74.2 us (level)
  no operation moved by 1% of the time
where the time goes in v11:
time: 74.2 us; the launch traced here: 73.6 us
  Pallas kernels  72.9 us (98%)
    pallas_call x1, Pallas kernels, body(): pl.pallas_call(kernel, out_shape=[V((2, CUT, 128), bf16), V((16, 16, SL),...  71.8 us

profile of v11, /device:TPU:1, one launch (start us, length us, event | category | flops | bytes accessed | tf_op | source)
XLA Modules:
  0.0 73.6 jit_solution(13920968128656965809)
XLA Ops:
  0.6 71.8 %exchange_compute.1 = (bf16[2,208,128]{2,1,0:T(8,128)(2,1)S(1)}, bf16[16,16,512]{2,1,0:T(8,128)(2,1)S(1)}, bf16[16,16,512]{2,1,0:T(8,128)(2,1)S(1)}, f32[16,1,512]{2,1,0:T(1,128)S(1)}) custom-call(bf16[394,1024]{1,0:T(8,128)(2,1)} %trunk.1, bf16[64,2048]{1,0:T(8,128)(2,1)} %exp.1, bf16[128,1024]{1,0:T(8,128)(2,1)} %shr.1, bf16[1,394,1024]{2,1,0:T(8,128)(2,1)} %cot.1, ...), custom_call_target="tpu_custom_call" | custom-call | tf_op jit(solution)/shard_map/exchange_compute/pallas_call | solution.py:592
  72.5 1.1 %write_outputs.1 = (bf16[64,394]{1,0:T(8,128)(2,1)}, f32[64,2048]{1,0:T(8,128)}, f32[128,1024]{1,0:T(8,128)}, f32[1,1024]{1,0:T(1,128)}, f32[1,2048]{1,0:T(1,128...) custom-call(bf16[2,208,128]{2,1,0:T(8,128)(2,1)S(1)} %get-tuple-element.20.tf, ...), custom_call_target="tpu_custom_call" | custom-call | tf_op jit(solution)/shard_map/write_outputs/pallas_call | solution.py:657
